TPU v7x, 256 devices: a whole 4x4x8 slice. The times are simulated.
256 devices in a mesh: sx: 4 (over z_hi), sy: 4 (over x), fq: 16 (over y, z_lo, core).
Axes of the slice: x: 4, y: 4, z: 8 (z_hi: 4, z_lo: 2; z = z_hi * 2 + z_lo), core: 2. Of those that a mesh axis runs over, the one named last changes fastest.
Arguments:
- spectra: bfloat16 [128, 2, 128, 64, 512], P('fq', None, 'sx', 'sy'), may hold values from -0.125 to 0.125
- noise_weight: float32 [512, 256], P(('sx', 'sy')), may hold values from 0.5 to 2
- class_map: int32 [128, 64], P('sx', 'sy'), may hold values from 0 to 7
- class_kappa: float32 [8], replicated, may hold values from 0.25 to 4
- solution: float32 [128, 512, 256], P('fq', ('sx', 'sy')), may hold values from -6 to 6
- residual: float32 [128, 512, 256], P('fq', ('sx', 'sy')), may hold values from -6 to 6
- direction: float32 [128, 512, 256], P('fq', ('sx', 'sy')), may hold values from -6 to 6
- step_length: float32 [128], P('fq'), may hold values from 0.2 to 1
- old_norm: float32 [128], P('fq'), may hold values from 131072 to 524288
Outputs:
- new_solution: float32 [128, 512, 256], P('fq', ('sx', 'sy'))
- new_residual: float32 [128, 512, 256], P('fq', ('sx', 'sy'))
- new_direction: float32 [128, 512, 256], P('fq', ('sx', 'sy'))
- new_norm: float32 [128], P('fq')
All inputs are finite; a program needn't handle non-finite values.
Results may differ from a plain program's by a relative error of at most 0.0022.
Values may be sent and summed in bfloat16 or wider, within the bound.
A program may use at most 128 MiB of HBM per device.

v0:
```python
import math

import jax
import jax.numpy as jnp
from jax import lax
from jax.sharding import PartitionSpec as P

SWEEPS = 4


HIGHEST = lax.Precision.HIGHEST


def side_by_side(arrays, axis, split_dim, concat_dim, along):
    ends, at = ([], 0)
    for a in arrays[:-1]:
        at += a.shape[along]
        ends.append(at)
    both = jnp.concatenate(arrays, axis=along)
    return tuple(
        jnp.split(
            lax.all_to_all(both, axis, split_axis=split_dim, concat_axis=concat_dim, tiled=True),
            ends,
            axis=along,
        )
    )


def turned_gather(arrays, axis, dims):
    turned = [jnp.moveaxis(a, dim, 0) for a, dim in zip(arrays, dims)]
    both = jnp.concatenate([t.reshape(len(t), -1) for t in turned], axis=1)
    whole, at, outs = (lax.all_gather(both, axis, axis=0, tiled=True), 0, [])
    for t, dim in zip(turned, dims):
        slab = whole[:, at : at + t[0].size].reshape(-1, *t.shape[1:])
        outs.append(jnp.moveaxis(slab, 0, dim))
        at += t[0].size
    return tuple(outs)


def padded_2(array, sides, width):
    edges = {}
    for axis, dim in sides:
        count, length = (lax.axis_size(axis), array.shape[dim])
        up = [(i, (i + 1) % count) for i in range(count - 1)]
        last = lax.slice_in_dim(array, length - width, length, axis=dim)
        initial = lax.slice_in_dim(array, 0, width, axis=dim)
        edges[dim] = (
            lax.ppermute(last, axis, up),
            lax.ppermute(initial, axis, [(b, a) for a, b in up]),
        )
    done = []
    for _, dim in sides:
        low, high = edges[dim]
        around = [(width, width) if d in done else (0, 0) for d in range(array.ndim)]
        array = jnp.concatenate([jnp.pad(low, around), array, jnp.pad(high, around)], axis=dim)
        done.append(dim)
    return array


def sent_to_all(array, axis):
    count = lax.axis_size(axis)
    return lax.all_to_all(
        jnp.broadcast_to(array[None], (count, *array.shape)), axis, 0, 0, tiled=True
    )


def over_copies(array, axis):
    everything = sent_to_all(array, axis)
    return jnp.sum(everything, axis=0)


def tables(freq_count, time_steps):
    freq_index = jnp.arange(freq_count, dtype=jnp.int32)[:, None]
    step_index = jnp.arange(time_steps, dtype=jnp.int32)[None, :]
    phases = (freq_index * step_index % time_steps).astype(jnp.float32) * (
        2.0 * math.pi / time_steps
    )
    factor = 1.0 / math.sqrt(time_steps)
    cosine_table = jnp.cos(phases) * factor
    sine_table = jnp.sin(phases) * factor
    doubling = jnp.where(jnp.arange(freq_count, dtype=jnp.int32) == 0, 1.0, 2.0).astype(jnp.float32)
    return (cosine_table, sine_table, doubling)


def neighbours(padded):
    return padded[2:, 1:-1] + padded[:-2, 1:-1] + padded[1:-1, 2:] + padded[1:-1, :-2]


def on_device(
    spectra,
    noise_weight,
    class_map,
    class_kappa,
    solution,
    residual,
    direction,
    step_length,
    old_norm,
):
    local_freqs = spectra.shape[0]
    cells_x = spectra.shape[2]
    cells_y = spectra.shape[3]
    local_cols, local_sensors, time_steps = direction.shape
    freq_count = local_freqs * lax.axis_size("fq")
    cosine_table, sine_table, doubling = tables(freq_count, time_steps)
    weighted = noise_weight[None] * direction
    spec_real = jnp.einsum("kst,ft->fks", weighted, cosine_table, precision=HIGHEST).astype(
        jnp.bfloat16
    )
    spec_imag = (-jnp.einsum("kst,ft->fks", weighted, sine_table, precision=HIGHEST)).astype(
        jnp.bfloat16
    )
    spec_real, spec_imag = side_by_side((spec_real, spec_imag), "fq", 0, 1, 2)
    all_cols = spec_real.shape[1]
    pieces = turned_gather((spec_real, spec_imag), ("sx", "sy"), (2, 2))
    rows_block = spectra
    real_part = rows_block[:, 0]
    imag_part = rows_block[:, 1]
    pattern = "fxys,fks->xyfk"
    part_real = jnp.einsum(
        pattern, real_part, pieces[0], preferred_element_type=jnp.float32
    ) + jnp.einsum(pattern, imag_part, pieces[1], preferred_element_type=jnp.float32)
    part_imag = jnp.einsum(
        pattern, real_part, pieces[1], preferred_element_type=jnp.float32
    ) - jnp.einsum(pattern, imag_part, pieces[0], preferred_element_type=jnp.float32)
    adjoint = jnp.stack([part_real, part_imag], 2)
    source = adjoint.reshape(cells_x, cells_y, 2 * local_freqs * all_cols)
    classes = jnp.arange(class_kappa.shape[0], dtype=jnp.int32)
    onehot = (class_map[:, :, None] == classes[None, None, :]).astype(jnp.float32)
    kappa_cells = jnp.sum(onehot * class_kappa[None, None, :], axis=2)[:, :, None]
    denom = 1.0 + 4.0 * kappa_cells
    smooth = source / denom
    for sweep_index in range(SWEEPS - 1):
        padded = padded_2(smooth.astype(jnp.bfloat16), (("sx", 0), ("sy", 1)), 1).astype(
            smooth.dtype
        )
        smooth = (source + kappa_cells * neighbours(padded)) / denom
    field_half = smooth.astype(jnp.bfloat16).reshape(cells_x, cells_y, 2, local_freqs, all_cols)
    field_real = field_half[:, :, 0]
    field_imag = field_half[:, :, 1]
    rows_block = spectra
    real_part = rows_block[:, 0]
    imag_part = rows_block[:, 1]
    pattern = "fxys,xyfk->sfk"
    out_real = jnp.einsum(
        pattern, real_part, field_real, preferred_element_type=jnp.float32
    ) - jnp.einsum(pattern, imag_part, field_imag, preferred_element_type=jnp.float32)
    out_imag = jnp.einsum(
        pattern, real_part, field_imag, preferred_element_type=jnp.float32
    ) + jnp.einsum(pattern, imag_part, field_real, preferred_element_type=jnp.float32)
    sensor_terms = lax.psum_scatter(
        jnp.stack([out_real, out_imag], 1), ("sx", "sy"), scatter_dimension=0, tiled=True
    )
    spectrum = lax.all_to_all(sensor_terms, "fq", split_axis=3, concat_axis=2, tiled=True)
    scaled_real = spectrum[:, 0] * doubling[None, :, None]
    scaled_imag = spectrum[:, 1] * doubling[None, :, None]
    returned = jnp.einsum("sfk,ft->kst", scaled_real, cosine_table, precision=HIGHEST) - jnp.einsum(
        "sfk,ft->kst", scaled_imag, sine_table, precision=HIGHEST
    )
    product = direction + noise_weight[None] * returned
    new_solution = solution + step_length[:, None, None] * direction
    new_residual = residual - step_length[:, None, None] * product
    new_norm = over_copies(jnp.sum(new_residual * new_residual, axis=(1, 2)), ("sx", "sy"))
    new_direction = new_residual + (new_norm / old_norm)[:, None, None] * direction
    return (new_solution, new_residual, new_direction, new_norm)


def solution(mesh):
    return jax.shard_map(
        on_device,
        mesh=mesh,
        in_specs=(
            P("fq", None, "sx", "sy", None),
            P(("sx", "sy"), None),
            P("sx", "sy"),
            P(),
            P("fq", ("sx", "sy"), None),
            P("fq", ("sx", "sy"), None),
            P("fq", ("sx", "sy"), None),
            P("fq"),
            P("fq"),
        ),
        out_specs=(
            P("fq", ("sx", "sy"), None),
            P("fq", ("sx", "sy"), None),
            P("fq", ("sx", "sy"), None),
            P("fq"),
        ),
        check_vma=False,
    )
```

profile of v0, /device:TPU:1, one launch (start us, length us, event | category | flops | bytes accessed | tf_op | source)
XLA Modules:
  0.0 349.6 jit_solution(10830805764259413589)
XLA Ops:
  7.2 1.8 convolution_convert_fusion
  9.1 1.8 fusion.42
  11.4 13.2 %all_to_all.42 = bf16[16,2,2048]{2,1,0:T(2,128)(2,1)S(1)} all-to-all(bf16[16,2,2048]{2,1,0:T(2,128)(2,1)S(1)} %reshape.63), channel_id=1, replica_groups=mesh['sx'=4,'sy'=4,'fq'=16] {'fq'}, dimensions={0} | all-to-all | bytes 262144 | tf_op jit(solution)/shard_map/all_to_all | solution.py:22
  26.2 6.0 %fusion.90 = (bf16[8,1,32,16,512]{4,3,2,1,0:T(8,128)(2,1)}, bf16[8,1,32,16,512]{4,3,2,1,0:T(8,128)(2,1)}) fusion(bf16[8,2,32,16,512]{4,3,2,1,0:T(8,128)(2,1)} %param.9), kind=kLoop, calls=%fused_computation.128 | loop fusion | bytes 16777216 | tf_op jit(solution)/shard_map/slice | solution.py:118
  32.2 51.7 %all-gather.2.cloned.1.call-done = bf16[512,2048]{1,0:T(8,128)(2,1)} async-done(((bf16[32,2048]{1,0:T(8,128)(2,1)}), bf16[512,2048]{1,0:T(8,128)(2,1)}) %all-gather.2.cloned.1.call-update) | async-done | bytes 2097168 | tf_op jit(solution)/shard_map/all_gather | solution.py:32
  83.8 1.7 fusion.98
  87.1 5.3 %fusion.30 = f32[8,128,32,16]{1,2,3,0:T(8,128)S(1)} fusion(bf16[8,128,512,1]{2,1,3,0:T(8,128)(2,1)S(1)} %bitcast.134, bf16[8,1,32,16,512]{4,3,2,1,0:T(8,128)(2,1)} %get-tuple-element.5), kind=kOutput, calls=%fused_computation.46 | convolution fusion | flops 536870912 | bytes 7340032 | tf_op jit(solution)/shard_map/fxys,fks->xyfk/dot_general | solution.py:120
  92.5 3.0 fusion.29
  95.4 2.8 add_bitcast_fusion
  98.2 3.1 subtract_bitcast_fusion
  101.8 4.6 %copy.71 = f32[32,16,2,8,128]{4,3,2,1,0:T(8,128)} copy(f32[32,16,2,8,128]{4,0,1,3,2:T(8,128)S(1)} %pad_maximum_fusion) | data formatting | bytes 8388608 | tf_op jit(solution)/shard_map/stack | solution.py:126
  106.4 4.9 %reshape.53 = f32[32,16,2048]{2,1,0:T(8,128)} reshape(f32[32,16,2,8,128]{4,3,2,1,0:T(8,128)} %copy.71) | data formatting | bytes 8388608 | tf_op jit(solution)/shard_map/reshape | solution.py:127
  111.3 2.8 divide_convert_fusion
  114.5 3.4 collective-permute-start
  117.9 1.3 collective-permute-start.3
  119.2 3.2 collective-permute-start.1
  122.4 1.3 collective-permute-start.2
  123.8 4.5 %collective-permute-done.2 = bf16[1,16,2048]{2,1,0:T(8,128)(2,1)S(1)} collective-permute-done((bf16[1,16,2048]{2,1,0:T(8,128)(2,1)S(1)}, bf16[1,16,2048]{2,1,0:T(8,128)(2,1)S(1)}, u32[]{:S(2)}, u32[]{:S(2)}) %collective-permute-start.2) | collective-permute-done | bytes 65568 | tf_op jit(solution)/shard_map/ppermute | solution.py:49
  128.3 1.8 fusion.19
  130.1 3.4 fusion.15
  133.9 4.0 %collective-permute-start.4 = (bf16[32,1,2048]{2,1,0:T(2,128)(2,1)S(1)}, bf16[32,1,2048]{2,1,0:T(2,128)(2,1)S(1)}, u32[]{:S(2)}, u32[]{:S(2)}) collective-permute-start(bf16[32,1,2048]{2,1,0:T(2,128)(2,1)S(1)} %get-tuple-element.14), channel_id=1, source_target_pairs={{0,16},{16,32},{32,48},{1,17},{17,33},{33,49},{2,18},{18,34},{34,5... | collective-permute-start | bytes 393224 | tf_op jit(solution)/shard_map/ppermute | solution.py:48
  137.9 1.3 collective-permute-start.7
  139.2 4.8 %collective-permute-start.5 = (bf16[1,16,2048]{2,1,0:T(8,128)(2,1)S(1)}, bf16[1,16,2048]{2,1,0:T(8,128)(2,1)S(1)}, u32[]{:S(2)}, u32[]{:S(2)}) collective-permute-start(bf16[1,16,2048]{2,1,0:T(8,128)(2,1)S(1)} %get-tuple-element.12), channel_id=1, source_target_pairs={{0,64},{64,128},{128,192},{1,65},{65,129},{129,193},{2,66},{66,130... | collective-permute-start | bytes 196616 | tf_op jit(solution)/shard_map/ppermute | solution.py:48
  144.0 1.3 collective-permute-start.6
  145.3 5.0 %collective-permute-done.6 = bf16[1,16,2048]{2,1,0:T(8,128)(2,1)S(1)} collective-permute-done((bf16[1,16,2048]{2,1,0:T(8,128)(2,1)S(1)}, bf16[1,16,2048]{2,1,0:T(8,128)(2,1)S(1)}, u32[]{:S(2)}, u32[]{:S(2)}) %collective-permute-start.6) | collective-permute-done | bytes 65568 | tf_op jit(solution)/shard_map/ppermute | solution.py:49
  150.3 1.8 fusion.21
  152.1 3.4 fusion.16
  155.9 1.3 collective-permute-start.11
  157.2 4.6 %collective-permute-start.8 = (bf16[32,1,2048]{2,1,0:T(2,128)(2,1)S(1)}, bf16[32,1,2048]{2,1,0:T(2,128)(2,1)S(1)}, u32[]{:S(2)}, u32[]{:S(2)}) collective-permute-start(bf16[32,1,2048]{2,1,0:T(2,128)(2,1)S(1)} %get-tuple-element.10), channel_id=1, source_target_pairs={{0,16},{16,32},{32,48},{1,17},{17,33},{33,49},{2,18},{18,34},{34,5... | collective-permute-start | bytes 393224 | tf_op jit(solution)/shard_map/ppermute | solution.py:48
  161.9 1.3 collective-permute-start.10
  163.2 4.9 %collective-permute-start.9 = (bf16[1,16,2048]{2,1,0:T(8,128)(2,1)S(1)}, bf16[1,16,2048]{2,1,0:T(8,128)(2,1)S(1)}, u32[]{:S(2)}, u32[]{:S(2)}) collective-permute-start(bf16[1,16,2048]{2,1,0:T(8,128)(2,1)S(1)} %get-tuple-element.8), channel_id=1, source_target_pairs={{0,64},{64,128},{128,192},{1,65},{65,129},{129,193},{2,66},{66,130... | collective-permute-start | bytes 196616 | tf_op jit(solution)/shard_map/ppermute | solution.py:48
  168.1 1.3 collective-permute-done.9
  169.4 1.8 fusion.23
  171.1 3.6 %fusion.17 = bf16[32,16,2048]{2,1,0:T(8,128)(2,1)S(1)} fusion(f32[32,16,2048]{2,1,0:T(8,128)S(1)} %copy-done.2, f32[34,18,2048]{2,1,0:T(8,128)S(1)} %fusion.23, f32[32,16]{1,0:T(8,128)S(1)} %copy.73, f32[32,16]{1,0:T(8,128)S(1)} %copy.72), kind=kLoop, calls=%fused_computation.33 | loop fusion | flops 7340032 | bytes 23072768 | tf_op jit(solution)/shard_map/convert_element_type | solution.py:138
  176.9 3.6 %fusion.28 = f32[8,128,512,1]{2,1,3,0:T(8,128)S(1)} fusion(bf16[8,1,32,16,512]{4,3,2,1,0:T(8,128)(2,1)S(1)} %copy-done.4, bf16[32,16,1,8,128]{4,3,2,1,0:T(8,128)(2,1)S(1)} %get-tuple-element.6), kind=kOutput, calls=%fused_computation.44 | convolution fusion | flops 536870912 | bytes 7340032 | tf_op jit(solution)/shard_map/fxys,xyfk->sfk/dot_general | solution.py:145
  180.5 3.6 %fusion.27 = f32[8,128,512,1]{2,1,3,0:T(8,128)S(1)} fusion(bf16[8,1,32,16,512]{4,3,2,1,0:T(8,128)(2,1)S(1)} %copy-done.4, bf16[32,16,1,8,128]{4,3,2,1,0:T(8,128)(2,1)S(1)} %get-tuple-element.7), kind=kOutput, calls=%fused_computation.43 | convolution fusion | flops 536870912 | bytes 7340032 | tf_op jit(solution)/shard_map/fxys,xyfk->sfk/dot_general | solution.py:148
  184.2 3.7 %fusion.36 = f32[512,1,8,128]{0,3,2,1:T(8,128)S(1)} fusion(f32[8,128,512,1]{2,1,3,0:T(8,128)S(1)} %fusion.28, bf16[8,1,32,16,512]{4,3,2,1,0:T(8,128)(2,1)S(1)} %copy-done.1, bf16[32,16,1,8,128]{4,3,2,1,0:T(8,128)(2,1)S(1)} %get-tuple-element.7), kind=kOutput, calls=%fused_computation.54 | convolution fusion | flops 537395200 | bytes 9437184 | tf_op jit(solution)/shard_map/fxys,xyfk->sfk/dot_general | solution.py:147
  187.8 3.9 %fusion.35 = f32[512,1,8,128]{0,3,2,1:T(8,128)S(1)} fusion(f32[8,128,512,1]{2,1,3,0:T(8,128)S(1)} %fusion.27, bf16[8,1,32,16,512]{4,3,2,1,0:T(8,128)(2,1)S(1)} %copy-done.1, bf16[32,16,1,8,128]{4,3,2,1,0:T(8,128)(2,1)S(1)} %get-tuple-element.6), kind=kOutput, calls=%fused_computation.52 | convolution fusion | flops 537395200 | bytes 9437184 | tf_op jit(solution)/shard_map/fxys,xyfk->sfk/dot_general | solution.py:150
  191.7 2.6 pad_maximum_fusion.1
  194.4 5.4 %copy.76 = f32[512,2,8,128]{3,2,1,0:T(8,128)} copy(f32[512,2,8,128]{0,3,2,1:T(8,128)} %pad_maximum_fusion.1) | data formatting | bytes 8388608 | tf_op jit(solution)/shard_map/stack | solution.py:152
  199.8 104.6 %reduce-scatter.2.cloned.1.call-done = f32[32,2,8,128]{3,2,1,0:T(8,128)} async-done(((f32[512,2,8,128]{3,2,1,0:T(8,128)}), f32[32,2,8,128]{3,2,1,0:T(8,128)}) %reduce-scatter.2.cloned.1.call-update) | async-done | bytes 262160 | tf_op jit(solution)/shard_map/reduce_scatter | solution.py:151
  304.5 1.5 copy.77
  307.1 6.3 %all-to-all-start.1 = ((f32[16,1,4096]{2,1,0:T(1,128)}), f32[16,1,4096]{2,1,0:T(1,128)S(1)}, u32[]{:S(2)}, u32[]{:S(2)}) async-start(f32[16,1,4096]{2,1,0:T(1,128)} %reshape.65), calls=%async_computation.2 | async-start | bytes 524288 | tf_op jit(solution)/shard_map/all_to_all | solution.py:154
  313.5 7.2 %all-to-all-done.1 = f32[16,1,4096]{2,1,0:T(1,128)S(1)} async-done(((f32[16,1,4096]{2,1,0:T(1,128)}), f32[16,1,4096]{2,1,0:T(1,128)S(1)}, u32[]{:S(2)}, u32[]{:S(2)}) %all-to-all-start.1) | async-done | bytes 262176 | tf_op jit(solution)/shard_map/all_to_all | solution.py:154
  321.2 1.3 reduce.1
  323.4 1.2 fusion.46
  324.7 1.3 multiply_reduce_fusion
  326.0 15.2 %all_to_all.43 = f32[16,1,8]{2,1,0:T(1,128)S(1)} all-to-all(f32[16,1,8]{2,1,0:T(1,128)S(1)} %broadcast_in_dim.12), channel_id=1, replica_groups=mesh['sx'=4,'sy'=4,'fq'=16] {'sx','sy'}, dimensions={0} | all-to-all | bytes 1024 | tf_op jit(solution)/shard_map/all_to_all | solution.py:62
  (77 shorter events, 11.3 us)
Async XLA Ops:
  7.2 18.8 %copy-start.10 = (s32[32,16]{0,1:T(8,128)S(1)}, s32[32,16]{0,1:T(8,128)}, u32[]{:S(2)}) copy-start(s32[32,16]{0,1:T(8,128)} %param.11) | copy-start | bytes 6148
  7.2 18.8 %copy-start.12 = (f32[8]{0:T(128)S(1)}, f32[8]{0:T(128)}, u32[]{:S(2)}) copy-start(f32[8]{0:T(128)} %param.12) | copy-start | bytes 100
  7.2 76.7 %all-gather.2.cloned.1.call-start = ((), (), s32[]{:S(2)}) async-start(), calls=%async_computation.4 | async-start | bytes 2228224 | tf_op jit(solution)/shard_map/all_gather | solution.py:32
  26.0 278.5 %reduce-scatter.2.cloned.1.call-start = ((), (), s32[]{:S(2)}) async-start(), calls=%async_computation.5 | async-start | bytes 4456448 | tf_op jit(solution)/shard_map/reduce_scatter | solution.py:151
  87.1 5.3 %copy-start.3 = (bf16[8,1,32,16,512]{4,3,2,1,0:T(8,128)(2,1)S(1)}, bf16[8,1,32,16,512]{4,3,2,1,0:T(8,128)(2,1)}, u32[]{:S(2)}) copy-start(bf16[8,1,32,16,512]{4,3,2,1,0:T(8,128)(2,1)} %get-tuple-element.5) | copy-start | bytes 12582916
  92.4 3.0 copy-start
  114.5 13.8 %collective-permute-start = (bf16[32,1,2048]{2,1,0:T(2,128)(2,1)S(1)}, bf16[32,1,2048]{2,1,0:T(2,128)(2,1)S(1)}, u32[]{:S(2)}, u32[]{:S(2)}) collective-permute-start(bf16[32,1,2048]{2,1,0:T(2,128)(2,1)S(1)} %get-tuple-element.18), channel_id=1, source_target_pairs={{0,16},{16,32},{32,48},{1,17},{17,33},{33,49},{2,18},{18,34},{34,5... | collective-permute-start | bytes 393224 | tf_op jit(solution)/shard_map/ppermute | solution.py:48
  117.9 10.4 %collective-permute-start.3 = (bf16[32,1,2048]{2,1,0:T(2,128)(2,1)S(1)}, bf16[32,1,2048]{2,1,0:T(2,128)(2,1)S(1)}, u32[]{:S(2)}, u32[]{:S(2)}) collective-permute-start(bf16[32,1,2048]{2,1,0:T(2,128)(2,1)S(1)} %get-tuple-element.19), channel_id=1, source_target_pairs={{16,0},{32,16},{48,32},{17,1},{33,17},{49,33},{18,2},{34,18},{50,3... | collective-permute-start | bytes 393224 | tf_op jit(solution)/shard_map/ppermute | solution.py:49
  119.2 4.6 %collective-permute-start.1 = (bf16[1,16,2048]{2,1,0:T(8,128)(2,1)S(1)}, bf16[1,16,2048]{2,1,0:T(8,128)(2,1)S(1)}, u32[]{:S(2)}, u32[]{:S(2)}) collective-permute-start(bf16[1,16,2048]{2,1,0:T(8,128)(2,1)S(1)} %get-tuple-element.16), channel_id=1, source_target_pairs={{0,64},{64,128},{128,192},{1,65},{65,129},{129,193},{2,66},{66,130... | collective-permute-start | bytes 196616 | tf_op jit(solution)/shard_map/ppermute | solution.py:48
  122.4 5.9 %collective-permute-start.2 = (bf16[1,16,2048]{2,1,0:T(8,128)(2,1)S(1)}, bf16[1,16,2048]{2,1,0:T(8,128)(2,1)S(1)}, u32[]{:S(2)}, u32[]{:S(2)}) collective-permute-start(bf16[1,16,2048]{2,1,0:T(8,128)(2,1)S(1)} %get-tuple-element.17), channel_id=1, source_target_pairs={{64,0},{128,64},{192,128},{65,1},{129,65},{193,129},{66,2},{130,66... | collective-permute-start | bytes 196616 | tf_op jit(solution)/shard_map/ppermute | solution.py:49
  123.8 6.3 %copy-start.2 = (f32[32,16,2048]{2,1,0:T(8,128)S(1)}, f32[32,16,2048]{2,1,0:T(8,128)}, u32[]{:S(2)}) copy-start(f32[32,16,2048]{2,1,0:T(8,128)} %reshape.53) | copy-start | bytes 12582916
  133.9 16.4 %collective-permute-start.4 = (bf16[32,1,2048]{2,1,0:T(2,128)(2,1)S(1)}, bf16[32,1,2048]{2,1,0:T(2,128)(2,1)S(1)}, u32[]{:S(2)}, u32[]{:S(2)}) collective-permute-start(bf16[32,1,2048]{2,1,0:T(2,128)(2,1)S(1)} %get-tuple-element.14), channel_id=1, source_target_pairs={{0,16},{16,32},{32,48},{1,17},{17,33},{33,49},{2,18},{18,34},{34,5... | collective-permute-start | bytes 393224 | tf_op jit(solution)/shard_map/ppermute | solution.py:48
  137.9 12.4 %collective-permute-start.7 = (bf16[32,1,2048]{2,1,0:T(2,128)(2,1)S(1)}, bf16[32,1,2048]{2,1,0:T(2,128)(2,1)S(1)}, u32[]{:S(2)}, u32[]{:S(2)}) collective-permute-start(bf16[32,1,2048]{2,1,0:T(2,128)(2,1)S(1)} %get-tuple-element.15), channel_id=1, source_target_pairs={{16,0},{32,16},{48,32},{17,1},{33,17},{49,33},{18,2},{34,18},{50,3... | collective-permute-start | bytes 393224 | tf_op jit(solution)/shard_map/ppermute | solution.py:49
  139.2 6.1 %collective-permute-start.5 = (bf16[1,16,2048]{2,1,0:T(8,128)(2,1)S(1)}, bf16[1,16,2048]{2,1,0:T(8,128)(2,1)S(1)}, u32[]{:S(2)}, u32[]{:S(2)}) collective-permute-start(bf16[1,16,2048]{2,1,0:T(8,128)(2,1)S(1)} %get-tuple-element.12), channel_id=1, source_target_pairs={{0,64},{64,128},{128,192},{1,65},{65,129},{129,193},{2,66},{66,130... | collective-permute-start | bytes 196616 | tf_op jit(solution)/shard_map/ppermute | solution.py:48
  144.0 6.3 %collective-permute-start.6 = (bf16[1,16,2048]{2,1,0:T(8,128)(2,1)S(1)}, bf16[1,16,2048]{2,1,0:T(8,128)(2,1)S(1)}, u32[]{:S(2)}, u32[]{:S(2)}) collective-permute-start(bf16[1,16,2048]{2,1,0:T(8,128)(2,1)S(1)} %get-tuple-element.13), channel_id=1, source_target_pairs={{64,0},{128,64},{192,128},{65,1},{129,65},{193,129},{66,2},{130,66... | collective-permute-start | bytes 196616 | tf_op jit(solution)/shard_map/ppermute | solution.py:49
  155.9 13.5 %collective-permute-start.11 = (bf16[32,1,2048]{2,1,0:T(2,128)(2,1)S(1)}, bf16[32,1,2048]{2,1,0:T(2,128)(2,1)S(1)}, u32[]{:S(2)}, u32[]{:S(2)}) collective-permute-start(bf16[32,1,2048]{2,1,0:T(2,128)(2,1)S(1)} %get-tuple-element.11), channel_id=1, source_target_pairs={{16,0},{32,16},{48,32},{17,1},{33,17},{49,33},{18,2},{34,18},{50,3... | collective-permute-start | bytes 393224 | tf_op jit(solution)/shard_map/ppermute | solution.py:49
  157.2 12.2 %collective-permute-start.8 = (bf16[32,1,2048]{2,1,0:T(2,128)(2,1)S(1)}, bf16[32,1,2048]{2,1,0:T(2,128)(2,1)S(1)}, u32[]{:S(2)}, u32[]{:S(2)}) collective-permute-start(bf16[32,1,2048]{2,1,0:T(2,128)(2,1)S(1)} %get-tuple-element.10), channel_id=1, source_target_pairs={{0,16},{16,32},{32,48},{1,17},{17,33},{33,49},{2,18},{18,34},{34,5... | collective-permute-start | bytes 393224 | tf_op jit(solution)/shard_map/ppermute | solution.py:48
  161.9 6.2 %collective-permute-start.10 = (bf16[1,16,2048]{2,1,0:T(8,128)(2,1)S(1)}, bf16[1,16,2048]{2,1,0:T(8,128)(2,1)S(1)}, u32[]{:S(2)}, u32[]{:S(2)}) collective-permute-start(bf16[1,16,2048]{2,1,0:T(8,128)(2,1)S(1)} %get-tuple-element.9), channel_id=1, source_target_pairs={{64,0},{128,64},{192,128},{65,1},{129,65},{193,129},{66,2},{130,66... | collective-permute-start | bytes 196616 | tf_op jit(solution)/shard_map/ppermute | solution.py:49
  163.2 6.2 %collective-permute-start.9 = (bf16[1,16,2048]{2,1,0:T(8,128)(2,1)S(1)}, bf16[1,16,2048]{2,1,0:T(8,128)(2,1)S(1)}, u32[]{:S(2)}, u32[]{:S(2)}) collective-permute-start(bf16[1,16,2048]{2,1,0:T(8,128)(2,1)S(1)} %get-tuple-element.8), channel_id=1, source_target_pairs={{0,64},{64,128},{128,192},{1,65},{65,129},{129,193},{2,66},{66,130... | collective-permute-start | bytes 196616 | tf_op jit(solution)/shard_map/ppermute | solution.py:48
  174.7 2.2 copy-start.4
  180.5 3.6 %copy-start.1 = (bf16[8,1,32,16,512]{4,3,2,1,0:T(8,128)(2,1)S(1)}, bf16[8,1,32,16,512]{4,3,2,1,0:T(8,128)(2,1)}, u32[]{:S(2)}) copy-start(bf16[8,1,32,16,512]{4,3,2,1,0:T(8,128)(2,1)} %get-tuple-element.4) | copy-start | bytes 12582916
  305.9 18.7 %copy-start.5 = (f32[8,32,256]{2,1,0:T(8,128)S(1)}, f32[8,32,256]{2,1,0:T(8,128)}, u32[]{:S(2)}) copy-start(f32[8,32,256]{2,1,0:T(8,128)} %param.15) | copy-start | bytes 786436
  306.0 18.7 %copy-start.7 = (f32[8,32,256]{2,1,0:T(8,128)S(1)}, f32[8,32,256]{2,1,0:T(8,128)}, u32[]{:S(2)}) copy-start(f32[8,32,256]{2,1,0:T(8,128)} %param.14) | copy-start | bytes 786436
  306.0 18.7 %copy-start.9 = (f32[32,256]{1,0:T(8,128)S(1)}, f32[32,256]{1,0:T(8,128)}, u32[]{:S(2)}) copy-start(f32[32,256]{1,0:T(8,128)} %param.10) | copy-start | bytes 98308
  306.0 18.7 %copy-start.11 = (f32[8]{0:T(128)S(1)}, f32[8]{0:T(128)}, u32[]{:S(2)}) copy-start(f32[8]{0:T(128)} %param.16) | copy-start | bytes 100
  307.1 13.5 %all-to-all-start.1 = ((f32[16,1,4096]{2,1,0:T(1,128)}), f32[16,1,4096]{2,1,0:T(1,128)S(1)}, u32[]{:S(2)}, u32[]{:S(2)}) async-start(f32[16,1,4096]{2,1,0:T(1,128)} %reshape.65), calls=%async_computation.2 | async-start | bytes 524288 | tf_op jit(solution)/shard_map/all_to_all | solution.py:154
  321.2 20.1 %copy-start.14 = (f32[8]{0:T(128)S(1)}, f32[8]{0:T(128)}, u32[]{:S(2)}) copy-start(f32[8]{0:T(128)} %param.17) | copy-start | bytes 100
  321.2 20.2 %copy-start.8 = (f32[8,32,256]{2,1,0:T(8,128)S(1)}, f32[8,32,256]{2,1,0:T(8,128)}, u32[]{:S(2)}) copy-start(f32[8,32,256]{2,1,0:T(8,128)} %param.13) | copy-start | bytes 786436
  326.0 16.3 %copy-start.6 = (f32[8,32,256]{2,1,0:T(8,128)}, f32[8,32,256]{2,1,0:T(8,128)S(1)}, u32[]{:S(2)}) copy-start(f32[8,32,256]{2,1,0:T(8,128)S(1)} %get-tuple-element.29) | copy-start | bytes 786436
  341.3 1.0 copy-start.13
Sparse Core Ops, SparseCore 0:
  26.1 57.7 all-gather.1
  199.9 104.4 reduce-scatter.1
where the time goes:
time: 354 us; the launch traced here: 350 us
  waiting for transfers between devices  174 us (49%)
  starting transfers between devices  39 us (11%)
  matrix products  35.1 us (10%)
  local copies, waits for them, and re-layouts  32.7 us (9%)
  blocking collectives  28.5 us (8%)
  other arithmetic  24.7 us (7%)
  between operations  15.1 us (4%)
    reduce_scatter x1, waiting for transfers between devices, on_device(): lax.psum_scatter(jnp.stack([out_real, out_imag], 1), ('sx', 'sy'), scatte...  105 us
    all_gather x1, waiting for transfers between devices, turned_gather(): whole, at, outs = (lax.all_gather(both, axis, axis=0, tiled=True), 0, [])  51.7 us
    ppermute x6, starting transfers between devices, padded_2(): lax.ppermute(last, axis, up)  24.9 us
    all_to_all x1, blocking collectives, sent_to_all(): lax.all_to_all(jnp.broadcast_to(array[None], (count, *array.shape)), axis...  15.2 us
    all_to_all x1, blocking collectives, side_by_side(): lax.all_to_all(both, axis, split_axis=split_dim, concat_axis=concat_dim,...  13.2 us
    convert_element_type x4, other arithmetic, on_device(): smooth.astype(jnp.bfloat16)  13.1 us
    ppermute x6, waiting for transfers between devices, padded_2(): lax.ppermute(initial, axis, [(b, a) for a, b in up])  9.52 us
    ppermute x6, starting transfers between devices, padded_2(): lax.ppermute(initial, axis, [(b, a) for a, b in up])  7.75 us
  transfers between devices with their start and end apart: 15, of which 6 were waited for; matrix products, arithmetic and copies ran while one was open for 2% of the time, Pallas kernels for 0%

commit v1 on v0

v1 whole, which is shorter than its diff:
```python
import functools
import math

import jax
import jax.numpy as jnp
import numpy as np
from jax import lax
from jax.experimental import pallas as pl
from jax.experimental.pallas import tpu as pltpu
from jax.sharding import PartitionSpec as P

MESH = pl.DeviceIdType.MESH
HIGHEST = lax.Precision.HIGHEST
BF, F32 = jnp.bfloat16, jnp.float32
PITCH = 24
NF = 8
G = 4


def tables(freq_count, time_steps, per_block):
    freq = np.arange(freq_count)
    phase = (freq[:, None] * np.arange(time_steps)[None, :] % time_steps) * (2.0 * math.pi / time_steps)
    factor = 1.0 / math.sqrt(time_steps)
    both = np.stack([np.cos(phase), -np.sin(phase)], axis=1) * factor
    doubled = both * np.where(freq == 0, 1.0, 2.0)[:, None, None]
    forward = both.reshape(2 * freq_count, time_steps).T
    back = doubled.reshape(2 * freq_count, time_steps)
    return forward.astype(np.float32), back.astype(np.float32)


def swapped(arrays, unit):
    arrays = list(arrays)
    lane = lax.broadcasted_iota(jnp.int32, arrays[0].shape, 1)
    bit = 1
    while bit < len(arrays):
        here = ((lane // unit) & bit) != 0
        for i in range(len(arrays)):
            if i & bit == 0:
                a, c = arrays[i], arrays[i | bit]
                arrays[i] = jnp.where(here, pltpu.roll(c, bit * unit, 1), a)
                arrays[i | bit] = jnp.where(here, c, pltpu.roll(a, 128 - bit * unit, 1))
        bit *= 2
    return arrays


def remote(src, dst, send, recv, device):
    return pltpu.make_async_remote_copy(
        src_ref=src, dst_ref=dst, send_sem=send, recv_sem=recv, device_id=device, device_id_type=MESH
    )


def kernel(
    dir_ref, res_ref, noise_ref, map_ref, kap_ref, step_ref, fwd_ref, back_ref, spectra_ref,
    new_res_ref, norm_ref,
    a, at, q, b0, p1, p2, kd, inv, out, sx_buf, fin, a2s, a2r, r2s, r2r,
    hxs, hxr, hys, hyr, rxf, rxd, rxc, rzf, rzd, rzc, ns, nr, fh,
    a_sem, as_sem, ar_sem, bs_sem, br_sem, ns_sem, nr_sem,
    zs, zr, xs, xr, hs, hr, rxs, rxr, rzs, rzr,
):
    sx, sy, fq = lax.axis_index("sx"), lax.axis_index("sy"), lax.axis_index("fq")
    tile = sx * G + sy

    def add(i, d, n):
        return lax.rem(i + d + n, n)

    def on_z(d):
        return (add(sx, d, G), sy, fq)

    def on_x(d):
        return (sx, add(sy, d, G), fq)

    def in_fq(d):
        return (sx, sy, add(fq, d, 16))

    def in_tiles(d):
        other = add(tile, d, 16)
        return (other // G, lax.rem(other, G), fq)

    barrier = pltpu.get_barrier_semaphore()
    for d in range(1, 16):
        pl.semaphore_signal(barrier, inc=1, device_id=in_fq(d), device_id_type=MESH)
        pl.semaphore_signal(barrier, inc=1, device_id=in_tiles(d), device_id_type=MESH)

    def a_copy(f):
        return pltpu.make_async_copy(spectra_ref.at[f], a.at[f], a_sem.at[f])

    for f in range(NF):
        a_copy(f).start()

    weighted = (dir_ref[...] * noise_ref[...][None]).reshape(256, 256)
    spec = jnp.dot(weighted, fwd_ref[...], preferred_element_type=F32, precision=HIGHEST)
    for half in range(2):
        part = [spec[32 * k : 32 * k + 32, 128 * half : 128 * half + 128] for k in range(8)]
        for i, chunk in enumerate(swapped(part, 16)):
            a2s[8 * half + i] = chunk.astype(BF)
    pl.semaphore_wait(barrier, 30)

    def a_exchange(d, src, dst, ss, rs):
        peer = in_fq(d)
        return remote(src.at[peer[2]], dst.at[fq], ss.at[d], rs.at[d], peer)

    def a_arrival(d, dst, ss, rs):
        peer = in_fq(-d)
        return remote(dst.at[peer[2]], dst.at[peer[2]], ss.at[d], rs.at[d], peer)

    for d in range(1, 16):
        a_exchange(d, a2s, a2r, as_sem, ar_sem).start()
    a2r[fq] = a2s[fq]

    classes = map_ref[...]
    kappa = jnp.zeros(classes.shape, F32)
    for c in range(8):
        kappa = jnp.where(classes == c, kap_ref[c], kappa)
    eye = lax.broadcasted_iota(jnp.int32, (16, 16), 0) == lax.broadcasted_iota(jnp.int32, (16, 16), 1)
    for x in range(32):
        row = jnp.broadcast_to(kappa[x : x + 1, :], (16, 16))
        column = jnp.sum(jnp.where(eye, row, 0.0), axis=1, keepdims=True)
        scale = 1.0 / (1.0 + 4.0 * column)
        inv[x] = jnp.broadcast_to(scale, (16, 128))
        kd[x] = jnp.broadcast_to(scale * column, (16, 128))

    zero_x = jnp.zeros((NF, 2, 16, 128), F32)
    zero_y = jnp.zeros((32, 128), F32)
    low_x, high_x = pl.ds(0, 16), pl.ds(33 * PITCH, 16)
    low_y, high_y = pl.ds(PITCH - 1, 32, stride=PITCH), pl.ds(PITCH + 16, 32, stride=PITCH)
    padded = (b0, p1, p2)

    @pl.when(sx == 0)
    def _():
        for p in padded:
            p[:, :, low_x, :] = zero_x

    @pl.when(sx == G - 1)
    def _():
        for p in padded:
            p[:, :, high_x, :] = zero_x

    @pl.when(sy == 0)
    def _():
        @pl.loop(0, NF)
        def _(f):
            for p in padded:
                for c in range(2):
                    p[f, c, low_y, :] = zero_y

    @pl.when(sy == G - 1)
    def _():
        @pl.loop(0, NF)
        def _(f):
            for p in padded:
                for c in range(2):
                    p[f, c, high_y, :] = zero_y

    for f in range(NF):
        a_copy(f).wait()
    for d in range(1, 16):
        a_arrival(d, a2r, as_sem, ar_sem).wait_recv()
    for i, block in enumerate(swapped([a2r[kb].astype(F32) for kb in range(16)], 1)):
        q[i // 2, sx, sy, i % 2] = block.astype(BF)

    def z_own(f, side):
        return remote(q.at[f, sx, sy], q.at[f, sx, sy], zs.at[f, side], zr.at[f, side], on_z(1 - 2 * side))

    def z_relay(f):
        side = lax.rem(f, 2)
        block = q.at[f, add(sx, 3 + 2 * side, G), sy]
        return remote(block, block, zs.at[f, 2], zr.at[f, 2], on_z(1 + 2 * side))

    def z_in(f, side):
        block = q.at[f, add(sx, 3 + 2 * side, G), sy]
        return remote(block, block, zs.at[f, side], zr.at[f, side], on_z(1))

    def z_far(f):
        block = q.at[f, add(sx, 2, G), sy]
        return remote(block, block, zs.at[f, 2], zr.at[f, 2], on_z(1))

    def x_own(f, side):
        block = q.at[f, :, sy]
        return remote(block, block, xs.at[f, side], xr.at[f, side], on_x(1 - 2 * side))

    def x_relay(f):
        side = lax.rem(f, 2)
        block = q.at[f, :, add(sy, 3 + 2 * side, G)]
        return remote(block, block, xs.at[f, 2], xr.at[f, 2], on_x(1 + 2 * side))

    def x_in(f, side):
        block = q.at[f, :, add(sy, 3 + 2 * side, G)]
        return remote(block, block, xs.at[f, side], xr.at[f, side], on_x(1))

    def x_far(f):
        block = q.at[f, :, add(sy, 2, G)]
        return remote(block, block, xs.at[f, 2], xr.at[f, 2], on_x(1))

    sides = ((sx > 0, on_z(-1)), (sx < G - 1, on_z(1)), (sy > 0, on_x(-1)), (sy < G - 1, on_x(1)))

    def h_out(j, f, side):
        s, r = (hxs, hxr) if side < 2 else (hys, hyr)
        return remote(
            s.at[j, f, side % 2], r.at[j, f, 1 - side % 2],
            hs.at[j, f, side], hr.at[j, f, side ^ 1], sides[side][1],
        )

    def h_in(j, f, side):
        r = hxr if side < 2 else hyr
        return remote(
            r.at[j, f, side % 2], r.at[j, f, side % 2], hs.at[j, f, side], hr.at[j, f, side], sides[side][1]
        )

    def send_edges(j, f, p):
        for c in range(2):
            hxs[j, f, 0, c] = p[f, c, pl.ds(PITCH, 16), :].astype(BF)
            hxs[j, f, 1, c] = p[f, c, pl.ds(32 * PITCH, 16), :].astype(BF)
            hys[j, f, 0, c] = p[f, c, pl.ds(PITCH, 32, stride=PITCH), :].astype(BF)
            hys[j, f, 1, c] = p[f, c, pl.ds(PITCH + 15, 32, stride=PITCH), :].astype(BF)
        for side in range(4):
            @pl.when(sides[side][0])
            def _():
                h_out(j, f, side).start()

    def take_halos(j, f, p):
        for side, rows in enumerate((low_x, high_x, low_y, high_y)):
            @pl.when(sides[side][0])
            def _():
                h_in(j, f, side).wait_recv()
                r = hxr if side < 2 else hyr
                for c in range(2):
                    p[f, c, rows, :] = r[j, f, side % 2, c].astype(F32)

    def adjoint(f):
        real = q[f, :, :, 0].reshape(512, 128)
        imag = q[f, :, :, 1].reshape(512, 128)
        acc = jnp.dot(a[f, 0], jnp.concatenate([real, imag], axis=1), preferred_element_type=F32)
        acc += jnp.dot(a[f, 1], jnp.concatenate([imag, -real], axis=1), preferred_element_type=F32)
        for x in range(32):
            for c in range(2):
                b0[f, c, pl.ds(PITCH * (x + 1), 16), :] = (
                    acc[16 * x : 16 * x + 16, 128 * c : 128 * c + 128] * inv[x]
                )
        send_edges(0, f, b0)

    @pl.loop(0, NF)
    def _(f):
        z_own(f, 0).start()
        z_own(f, 1).start()

    @pl.loop(0, NF + 3)
    def _(i):
        @pl.when(i < NF)
        def _():
            z_in(i, lax.rem(i, 2)).wait_recv()
            z_relay(i).start()

        @pl.when((i >= 1) & (i < NF + 1))
        def _():
            f = i - 1
            z_in(f, 1 - lax.rem(f, 2)).wait_recv()
            z_far(f).wait_recv()
            x_own(f, 0).start()
            x_own(f, 1).start()

        @pl.when((i >= 2) & (i < NF + 2))
        def _():
            f = i - 2
            x_in(f, lax.rem(f, 2)).wait_recv()
            x_relay(f).start()

        @pl.when(i < NF)
        def _():
            for c in range(2):
                at[i, c] = a[i, c].T

        @pl.when(i >= 3)
        def _():
            f = i - 3
            x_in(f, 1 - lax.rem(f, 2)).wait_recv()
            x_far(f).wait_recv()
            adjoint(f)

    def swept(f, c, x, p):
        base = PITCH * (x + 1)
        around = (
            p[f, c, pl.ds(base - PITCH, 16), :] + p[f, c, pl.ds(base + PITCH, 16), :]
            + p[f, c, pl.ds(base - 1, 16), :] + p[f, c, pl.ds(base + 1, 16), :]
        )
        return b0[f, c, pl.ds(base, 16), :] + kd[x] * around

    for j, (before, after) in enumerate(((b0, p1), (p1, p2))):
        @pl.loop(0, NF)
        def _(f):
            take_halos(j, f, before)
            for x in range(32):
                for c in range(2):
                    after[f, c, pl.ds(PITCH * (x + 1), 16), :] = swept(f, c, x, before)
            send_edges(j + 1, f, after)

    def forward(f):
        take_halos(2, f, p2)
        for x in range(32):
            for c in range(2):
                fh[c, pl.ds(16 * x, 16), :] = swept(f, c, x, p2).astype(BF)
        real, imag = fh[0], fh[1]
        acc = jnp.dot(at[f, 0], jnp.concatenate([real, imag], axis=1), preferred_element_type=F32)
        acc += jnp.dot(at[f, 1], jnp.concatenate([-imag, real], axis=1), preferred_element_type=F32)
        for t in range(16):
            for c in range(2):
                out[f, t % G, t // G, c] = acc[32 * t : 32 * t + 32, 128 * c : 128 * c + 128].astype(BF)

    def way(f):
        return 1 + 2 * lax.rem(f, 2)

    def back(f):
        return 3 - 2 * lax.rem(f, 2)

    def x_sum(f, kind):
        d, to, land = ((2, way(f), rxf), (back(f), back(f), rxd), (way(f), way(f), rxc))[kind]
        return remote(out.at[f, add(sy, d, G)], land.at[f], rxs.at[f, kind], rxr.at[f, kind], on_x(to))

    def z_sum(f, kind):
        d, to, land = ((2, way(f), rzf), (back(f), back(f), rzd), (way(f), way(f), rzc))[kind]
        return remote(sx_buf.at[f, add(sx, d, G)], land.at[f], rzs.at[f, kind], rzr.at[f, kind], on_z(to))

    @pl.loop(0, NF + 4)
    def _(i):
        @pl.when(i < NF)
        def _():
            forward(i)
            x_sum(i, 0).start()
            x_sum(i, 1).start()

        @pl.when((i >= 1) & (i < NF + 1))
        def _():
            f = i - 1
            x_sum(f, 0).wait_recv()
            there = add(sy, way(f), G)
            out[f, there] = (out[f, there].astype(F32) + rxf[f].astype(F32)).astype(BF)
            x_sum(f, 2).start()

        @pl.when((i >= 2) & (i < NF + 2))
        def _():
            f = i - 2
            x_sum(f, 1).wait_recv()
            x_sum(f, 2).wait_recv()
            sx_buf[f] = (out[f, sy].astype(F32) + rxd[f].astype(F32) + rxc[f].astype(F32)).astype(BF)
            z_sum(f, 0).start()
            z_sum(f, 1).start()

        @pl.when((i >= 3) & (i < NF + 3))
        def _():
            f = i - 3
            z_sum(f, 0).wait_recv()
            there = add(sx, way(f), G)
            sx_buf[f, there] = (sx_buf[f, there].astype(F32) + rzf[f].astype(F32)).astype(BF)
            z_sum(f, 2).start()

        @pl.when(i >= 4)
        def _():
            f = i - 4
            z_sum(f, 1).wait_recv()
            z_sum(f, 2).wait_recv()
            fin[f] = sx_buf[f, sx].astype(F32) + rzd[f].astype(F32) + rzc[f].astype(F32)

    for kb, chunk in enumerate(swapped([fin[i // 2, i % 2] for i in range(16)], 1)):
        r2s[kb] = chunk.astype(BF)
    for d in range(1, 16):
        a_exchange(d, r2s, r2r, bs_sem, br_sem).start()
    r2r[fq] = r2s[fq]
    for d in range(1, 16):
        a_arrival(d, r2r, bs_sem, br_sem).wait_recv()
    halves = []
    for half in range(2):
        part = swapped([r2r[8 * half + i].astype(F32) for i in range(8)], 16)
        halves.append(jnp.concatenate(part, axis=0))
    returned = jnp.dot(
        jnp.concatenate(halves, axis=1), back_ref[...], preferred_element_type=F32, precision=HIGHEST
    )

    for k in range(8):
        product = dir_ref[k] + noise_ref[...] * returned[32 * k : 32 * k + 32]
        new = res_ref[k] - step_ref[k] * product
        new_res_ref[k] = new
        total = jnp.sum(jnp.sum(new * new, axis=1, keepdims=True), axis=0, keepdims=True)
        ns[k : k + 1, :] = jnp.broadcast_to(total, (1, 128))

    def n_copy(d):
        return remote(ns, nr.at[d], ns_sem.at[d], nr_sem.at[d], in_tiles(d))

    for d in range(1, 16):
        n_copy(d).start()
    norm = ns[...]
    for d in range(1, 16):
        n_copy(d).wait_recv()
        norm += nr[d]
    norm_ref[...] = norm

    for d in range(1, 16):
        a_exchange(d, a2s, a2r, as_sem, ar_sem).wait_send()
        a_exchange(d, r2s, r2r, bs_sem, br_sem).wait_send()
        n_copy(d).wait_send()

    @pl.loop(0, NF)
    def _(f):
        for side in range(2):
            z_own(f, side).wait_send()
            x_own(f, side).wait_send()
        z_relay(f).wait_send()
        x_relay(f).wait_send()
        for kind in range(3):
            x_sum(f, kind).wait_send()
            z_sum(f, kind).wait_send()
        for j in range(3):
            for side in range(4):
                @pl.when(sides[side][0])
                def _():
                    h_out(j, f, side).wait_send()


def on_device(
    spectra, noise_weight, class_map, class_kappa, solution, residual, direction, step_length, old_norm
):
    forward_table, back_table = tables(128, 256, NF)
    vmem = pl.BlockSpec(memory_space=pltpu.VMEM)
    smem = pl.BlockSpec(memory_space=pltpu.SMEM)
    dma = pltpu.SemaphoreType.DMA
    field = pltpu.VMEM((NF, 2, 34 * PITCH, 128), F32)
    chunks = pltpu.VMEM((16, 32, 128), BF)
    x_part = pltpu.VMEM((NF, G, 2, 32, 128), BF)
    z_part = pltpu.VMEM((NF, 2, 32, 128), BF)
    new_residual, norm = pl.pallas_call(
        kernel,
        out_shape=(
            jax.ShapeDtypeStruct(residual.shape, F32),
            jax.ShapeDtypeStruct((8, 128), F32),
        ),
        in_specs=[vmem] * 4 + [smem] * 2 + [vmem] * 2 + [pl.BlockSpec(memory_space=pl.ANY)],
        out_specs=(vmem, vmem),
        scratch_shapes=[
            pltpu.VMEM((NF, 2, 512, 512), BF),
            pltpu.VMEM((NF, 2, 512, 512), BF),
            pltpu.VMEM((NF, G, G, 2, 32, 128), BF),
            field, field, field,
            pltpu.VMEM((32, 16, 128), F32), pltpu.VMEM((32, 16, 128), F32),
            pltpu.VMEM((NF, G, G, 2, 32, 128), BF),
            x_part,
            pltpu.VMEM((NF, 2, 32, 128), F32),
            chunks, chunks, chunks, chunks,
            pltpu.VMEM((3, NF, 2, 2, 16, 128), BF), pltpu.VMEM((3, NF, 2, 2, 16, 128), BF),
            pltpu.VMEM((3, NF, 2, 2, 32, 128), BF), pltpu.VMEM((3, NF, 2, 2, 32, 128), BF),
            x_part, x_part, x_part, z_part, z_part, z_part,
            pltpu.VMEM((8, 128), F32), pltpu.VMEM((16, 8, 128), F32),
            pltpu.VMEM((2, 512, 128), BF),
            dma((NF,)),
            dma((16,)), dma((16,)), dma((16,)), dma((16,)), dma((16,)), dma((16,)),
            dma((NF, 3)), dma((NF, 3)), dma((NF, 3)), dma((NF, 3)),
            dma((3, NF, 4)), dma((3, NF, 4)),
            dma((NF, 3)), dma((NF, 3)), dma((NF, 3)), dma((NF, 3)),
        ],
        compiler_params=pltpu.CompilerParams(
            collective_id=0, has_side_effects=True, vmem_limit_bytes=62 * 1024 * 1024
        ),
        name="hessian_step",
    )(
        direction, residual, noise_weight, class_map, class_kappa, step_length,
        jnp.asarray(forward_table), jnp.asarray(back_table), spectra.reshape(NF, 2, 512, 512),
    )
    new_norm = norm[:, 0]
    new_solution = solution + step_length[:, None, None] * direction
    new_direction = new_residual + (new_norm / old_norm)[:, None, None] * direction
    return (new_solution, new_residual, new_direction, new_norm)


def solution(mesh):
    columns = P("fq", ("sx", "sy"), None)
    return jax.shard_map(
        on_device,
        mesh=mesh,
        in_specs=(
            P("fq", None, "sx", "sy", None), P(("sx", "sy"), None), P("sx", "sy"), P(),
            columns, columns, columns, P("fq"), P("fq"),
        ),
        out_specs=(columns, columns, columns, P("fq")),
        check_vma=False,
    )
```

time: 354 us -> 122 us (0.34); the launches traced: 350 us -> 122 us
  waiting for transfers between devices: 174 us -> 0 us
  Pallas kernels: 0 us -> 115 us
  starting transfers between devices: 39 us -> 0 us
  matrix products: 35.1 us -> 0 us
  local copies, waits for them, and re-layouts: 32.7 us -> 3.92 us
  blocking collectives: 28.5 us -> 0 us
  other arithmetic: 24.7 us -> 1.86 us
  between operations: 15.1 us -> 0.71 us
    pallas_call x0 -> x1, Pallas kernels: none -> 115 us  [on_device(): pl.pallas_call(kernel, out_shape=(jax.ShapeDtypeStruct(residual.shape, F3...]
    reduce_scatter x1 -> x0, waiting for transfers between devices: 105 us -> none  [on_device(): lax.psum_scatter(jnp.stack([out_real, out_imag], 1), ('sx', 'sy'), scatte...]
    all_gather x1 -> x0, waiting for transfers between devices: 51.7 us -> none  [turned_gather(): whole, at, outs = (lax.all_gather(both, axis, axis=0, tiled=True), 0, [])]
    dot_general x12 -> x0, matrix products: 35.1 us -> none  [the longest x1 5.3 us: on_device(): jnp.einsum(pattern, real_part, pieces[0], preferred_element_type=jnp.floa...]
    ppermute x12 -> x0, starting transfers between devices: 32.6 us -> none  [the longest x6 24.9 us: padded_2(): lax.ppermute(last, axis, up)]
    all_to_all x2 -> x0, blocking collectives: 28.5 us -> none  [the longest x1 15.2 us: sent_to_all(): lax.all_to_all(jnp.broadcast_to(array[None], (count, *array.shape)), axis...]
    convert_element_type x7 -> x0, other arithmetic: 18.3 us -> none  [the longest x4 13.1 us: on_device(): smooth.astype(jnp.bfloat16)]
    ppermute x12 -> x0, waiting for transfers between devices: 10.8 us -> none  [the longest x6 9.52 us: padded_2(): lax.ppermute(initial, axis, [(b, a) for a, b in up])]
  transfers between devices with their start and end apart: 15 -> 0, of which waited for: 6 -> 0; matrix products, arithmetic and copies ran while one was open for 2% -> 0% of each run, Pallas kernels for 0% -> 0%
where the time goes in v1:
time: 122 us
  Pallas kernels  115 us (94%)
  local copies, waits for them, and re-layouts  3.92 us (3%)
  other arithmetic  1.86 us (2%)
    pallas_call x1, Pallas kernels, on_device(): pl.pallas_call(kernel, out_shape=(jax.ShapeDtypeStruct(residual.shape, F3...  115 us
    unnamed x12, local copies, waits for them, and re-layouts  3.13 us

profile of v1, /device:TPU:1, one launch (start us, length us, event | category | flops | bytes accessed | tf_op | source)
XLA Modules:
  0.0 121.8 jit_solution(9838271826226561242)
XLA Ops:
  0.6 0.0 copy-start
  0.6 0.0 copy-start.2
  0.7 0.0 copy-start.4
  0.7 0.0 copy-start.1
  0.7 1.4 %copy.16.map_ref = s32[32,16]{1,0:T(8,128)} copy(s32[32,16]{0,1:T(8,128)} %param.13) | data formatting | bytes 4096 | tf_op args[2]
  2.1 115.4 %hessian_step.1 = (f32[8,32,256]{2,1,0:T(8,128)}, f32[8,128]{1,0:T(8,128)}) custom-call(f32[8,32,256]{2,1,0:T(8,128)} %dir_ref.1, f32[8,32,256]{2,1,0:T(8,128)} %res_ref.1, f32[32,256]{1,0:T(8,128)} %noise_ref.1, s32[32,16]{1,0:T(8,128)} %copy.16.map_ref, f32[8]{0:T(128)} %kap_ref.1, f32[8]{0:T(128)} %step_ref.1, f32[256,256]{1,0:T(8,128)} %constant.4.clone.fwd_ref, ...), custom_call_target="tpu_custom_call" | custom-call | tf_op jit(solution)/shard_map/hessian_step/pallas_call | solution.py:428
  117.5 0.8 slice_reduce_fusion
  118.3 0.0 copy-done.4
  118.3 0.0 copy-start.3
  118.3 0.0 copy-done
  118.3 0.0 copy-done.2
  118.3 0.0 copy-done.1
  118.3 1.9 %multiply_add_fusion = (f32[8,32,256]{2,1,0:T(8,128)}, f32[8,32,256]{2,1,0:T(8,128)}) fusion(f32[8,32,256]{2,1,0:T(8,128)} %get-tuple-element.15, f32[8,32,256]{2,1,0:T(8,128)S(1)} %copy-done, f32[8]{0:T(128)S(1)} %div.3, f32[8,32,256]{2,1,0:T(8,128)S(1)} %copy-done.1, f32[8]{0:T(128)S(1)} %copy-done.2), kind=kLoop, calls=%fused_computation | loop fusion | flops 262144 | bytes 1310784 | tf_op jit(solution)/shard_map/add | solution.py:467
  120.2 1.7 %copy.18 = f32[8,32,256]{2,1,0:T(8,128)} copy(f32[8,32,256]{2,1,0:T(8,128)} %get-tuple-element.15) | data formatting | bytes 524288
  121.8 0.0 copy-done.3
  (1 shorter events, 0.0 us)
Async XLA Ops:
  0.6 117.7 %copy-start = (f32[8,32,256]{2,1,0:T(8,128)S(1)}, f32[8,32,256]{2,1,0:T(8,128)}, u32[]{:S(2)}) copy-start(f32[8,32,256]{2,1,0:T(8,128)} %dir_ref.1) | copy-start | bytes 786436
  0.6 117.7 %copy-start.2 = (f32[8]{0:T(128)S(1)}, f32[8]{0:T(128)}, u32[]{:S(2)}) copy-start(f32[8]{0:T(128)} %step_ref.1) | copy-start | bytes 100
  0.7 117.6 %copy-start.4 = (f32[8]{0:T(128)S(1)}, f32[8]{0:T(128)}, u32[]{:S(2)}) copy-start(f32[8]{0:T(128)} %param.19) | copy-start | bytes 100
  0.7 117.6 %copy-start.1 = (f32[8,32,256]{2,1,0:T(8,128)S(1)}, f32[8,32,256]{2,1,0:T(8,128)}, u32[]{:S(2)}) copy-start(f32[8,32,256]{2,1,0:T(8,128)} %param.15) | copy-start | bytes 786436
  118.3 3.6 %copy-start.3 = (f32[8]{0:T(128)}, f32[8]{0:T(128)S(1)}, u32[]{:S(2)}) copy-start(f32[8]{0:T(128)S(1)} %slice_reduce_fusion) | copy-start | bytes 100

commit v2 on v1

--- a/solution.py
+++ b/solution.py
@@ -15,6 +15,8 @@
 PITCH = 24
 NF = 8
 G = 4
+FAR, PASS, PASS_FAR, ADJOINT, SWEEP1, SWEEP2, FORWARD, X_RELAY, X_TOTAL, Z_RELAY = 1, 2, 3, 5, 8, 11, 14, 17, 20, 23
+OWN_ROW, OWN_RELAY = NF + X_RELAY - 1, NF + X_TOTAL - 1
 
 
 def tables(freq_count, time_steps, per_block):
@@ -50,8 +52,9 @@
 
 
 def kernel(
-    dir_ref, res_ref, noise_ref, map_ref, kap_ref, step_ref, fwd_ref, back_ref, spectra_ref,
-    new_res_ref, norm_ref,
+    dir_hbm, noise_hbm, fwd_hbm, map_hbm, back_hbm, res_hbm, kap_ref, step_ref, spectra_ref,
+    delta_hbm, norm_ref,
+    dir_ref, noise_ref, fwd_ref, map_ref, back_ref, res_ref, delta, in_sem, out_sem,
     a, at, q, b0, p1, p2, kd, inv, out, sx_buf, fin, a2s, a2r, r2s, r2r,
     hxs, hxr, hys, hyr, rxf, rxd, rxc, rzf, rzd, rzc, ns, nr, fh,
     a_sem, as_sem, ar_sem, bs_sem, br_sem, ns_sem, nr_sem,
@@ -81,9 +84,21 @@
         pl.semaphore_signal(barrier, inc=1, device_id=in_fq(d), device_id_type=MESH)
         pl.semaphore_signal(barrier, inc=1, device_id=in_tiles(d), device_id_type=MESH)
 
+    loads = [
+        pltpu.make_async_copy(src, dst, in_sem.at[i])
+        for i, (src, dst) in enumerate((
+            (dir_hbm, dir_ref), (noise_hbm, noise_ref), (fwd_hbm, fwd_ref),
+            (map_hbm, map_ref), (back_hbm, back_ref), (res_hbm, res_ref),
+        ))
+    ]
+    for load in loads:
+        load.start()
+
     def a_copy(f):
         return pltpu.make_async_copy(spectra_ref.at[f], a.at[f], a_sem.at[f])
 
+    for load in loads[:3]:
+        load.wait()
     for f in range(NF):
         a_copy(f).start()
 
@@ -107,17 +122,16 @@
         a_exchange(d, a2s, a2r, as_sem, ar_sem).start()
     a2r[fq] = a2s[fq]
 
+    loads[3].wait()
     classes = map_ref[...]
     kappa = jnp.zeros(classes.shape, F32)
     for c in range(8):
         kappa = jnp.where(classes == c, kap_ref[c], kappa)
-    eye = lax.broadcasted_iota(jnp.int32, (16, 16), 0) == lax.broadcasted_iota(jnp.int32, (16, 16), 1)
+    scale = 1.0 / (1.0 + 4.0 * kappa)
+    ratio = scale * kappa
     for x in range(32):
-        row = jnp.broadcast_to(kappa[x : x + 1, :], (16, 16))
-        column = jnp.sum(jnp.where(eye, row, 0.0), axis=1, keepdims=True)
-        scale = 1.0 / (1.0 + 4.0 * column)
-        inv[x] = jnp.broadcast_to(scale, (16, 128))
-        kd[x] = jnp.broadcast_to(scale * column, (16, 128))
+        inv[x] = jnp.broadcast_to(scale[:, x : x + 1], (16, 128))
+        kd[x] = jnp.broadcast_to(ratio[:, x : x + 1], (16, 128))
 
     zero_x = jnp.zeros((NF, 2, 16, 128), F32)
     zero_y = jnp.zeros((32, 128), F32)
@@ -174,22 +188,22 @@
         block = q.at[f, add(sx, 2, G), sy]
         return remote(block, block, zs.at[f, 2], zr.at[f, 2], on_z(1))
 
-    def x_own(f, side):
-        block = q.at[f, :, sy]
-        return remote(block, block, xs.at[f, side], xr.at[f, side], on_x(1 - 2 * side))
-
-    def x_relay(f):
+    def x_own(f, row, side):
+        block = q.at[f, row, sy]
+        return remote(block, block, xs.at[f, side, row], xr.at[f, side, row], on_x(1 - 2 * side))
+
+    def x_relay(f, row):
         side = lax.rem(f, 2)
-        block = q.at[f, :, add(sy, 3 + 2 * side, G)]
-        return remote(block, block, xs.at[f, 2], xr.at[f, 2], on_x(1 + 2 * side))
-
-    def x_in(f, side):
-        block = q.at[f, :, add(sy, 3 + 2 * side, G)]
-        return remote(block, block, xs.at[f, side], xr.at[f, side], on_x(1))
-
-    def x_far(f):
-        block = q.at[f, :, add(sy, 2, G)]
-        return remote(block, block, xs.at[f, 2], xr.at[f, 2], on_x(1))
+        block = q.at[f, row, add(sy, 3 + 2 * side, G)]
+        return remote(block, block, xs.at[f, 2, row], xr.at[f, 2, row], on_x(1 + 2 * side))
+
+    def x_in(f, row, side):
+        block = q.at[f, row, add(sy, 3 + 2 * side, G)]
+        return remote(block, block, xs.at[f, side, row], xr.at[f, side, row], on_x(1))
+
+    def x_far(f, row):
+        block = q.at[f, row, add(sy, 2, G)]
+        return remote(block, block, xs.at[f, 2, row], xr.at[f, 2, row], on_x(1))
 
     sides = ((sx > 0, on_z(-1)), (sx < G - 1, on_z(1)), (sy > 0, on_x(-1)), (sy < G - 1, on_x(1)))
 
@@ -240,41 +254,17 @@
 
     @pl.loop(0, NF)
     def _(f):
-        z_own(f, 0).start()
-        z_own(f, 1).start()
-
-    @pl.loop(0, NF + 3)
-    def _(i):
-        @pl.when(i < NF)
-        def _():
-            z_in(i, lax.rem(i, 2)).wait_recv()
-            z_relay(i).start()
-
-        @pl.when((i >= 1) & (i < NF + 1))
-        def _():
-            f = i - 1
-            z_in(f, 1 - lax.rem(f, 2)).wait_recv()
-            z_far(f).wait_recv()
-            x_own(f, 0).start()
-            x_own(f, 1).start()
-
-        @pl.when((i >= 2) & (i < NF + 2))
-        def _():
-            f = i - 2
-            x_in(f, lax.rem(f, 2)).wait_recv()
-            x_relay(f).start()
-
-        @pl.when(i < NF)
-        def _():
-            for c in range(2):
-                at[i, c] = a[i, c].T
-
-        @pl.when(i >= 3)
-        def _():
-            f = i - 3
-            x_in(f, 1 - lax.rem(f, 2)).wait_recv()
-            x_far(f).wait_recv()
-            adjoint(f)
+        for side in range(2):
+            z_own(f, side).start()
+        for side in range(2):
+            x_own(f, sx, side).start()
+
+    def pass_on(f, row):
+        x_in(f, row, lax.rem(f, 2)).wait_recv()
+        x_relay(f, row).start()
+
+    def row_of(side):
+        return add(sx, 3 + 2 * side, G)
 
     def swept(f, c, x, p):
         base = PITCH * (x + 1)
@@ -284,14 +274,12 @@
         )
         return b0[f, c, pl.ds(base, 16), :] + kd[x] * around
 
-    for j, (before, after) in enumerate(((b0, p1), (p1, p2))):
-        @pl.loop(0, NF)
-        def _(f):
-            take_halos(j, f, before)
-            for x in range(32):
-                for c in range(2):
-                    after[f, c, pl.ds(PITCH * (x + 1), 16), :] = swept(f, c, x, before)
-            send_edges(j + 1, f, after)
+    def sweep(j, f, before, after):
+        take_halos(j, f, before)
+        for x in range(32):
+            for c in range(2):
+                after[f, c, pl.ds(PITCH * (x + 1), 16), :] = swept(f, c, x, before)
+        send_edges(j + 1, f, after)
 
     def forward(f):
         take_halos(2, f, p2)
@@ -303,7 +291,7 @@
         acc += jnp.dot(at[f, 1], jnp.concatenate([-imag, real], axis=1), preferred_element_type=F32)
         for t in range(16):
             for c in range(2):
-                out[f, t % G, t // G, c] = acc[32 * t : 32 * t + 32, 128 * c : 128 * c + 128].astype(BF)
+                out[f, t % G, lax.rem(t // G + G - sx, G), c] = acc[32 * t : 32 * t + 32, 128 * c : 128 * c + 128].astype(BF)
 
     def way(f):
         return 1 + 2 * lax.rem(f, 2)
@@ -311,53 +299,131 @@
     def back(f):
         return 3 - 2 * lax.rem(f, 2)
 
-    def x_sum(f, kind):
+    rest = (pl.ds(1, G - 1), pl.ds(0, 1))
+
+    def x_sum(f, kind, part):
         d, to, land = ((2, way(f), rxf), (back(f), back(f), rxd), (way(f), way(f), rxc))[kind]
-        return remote(out.at[f, add(sy, d, G)], land.at[f], rxs.at[f, kind], rxr.at[f, kind], on_x(to))
+        return remote(
+            out.at[f, add(sy, d, G), rest[part]], land.at[f, rest[part]],
+            rxs.at[f, kind, part], rxr.at[f, kind, part], on_x(to),
+        )
 
     def z_sum(f, kind):
         d, to, land = ((2, way(f), rzf), (back(f), back(f), rzd), (way(f), way(f), rzc))[kind]
-        return remote(sx_buf.at[f, add(sx, d, G)], land.at[f], rzs.at[f, kind], rzr.at[f, kind], on_z(to))
-
-    @pl.loop(0, NF + 4)
+        return remote(sx_buf.at[f, d], land.at[f], rzs.at[f, kind], rzr.at[f, kind], on_z(to))
+
+    def x_relay_sum(f, part):
+        x_sum(f, 0, part).wait_recv()
+        there, rows = add(sy, way(f), G), rest[part]
+        out[f, there, rows] = (out[f, there, rows].astype(F32) + rxf[f, rows].astype(F32)).astype(BF)
+        x_sum(f, 2, part).start()
+
+    def x_total(f, part):
+        x_sum(f, 1, part).wait_recv()
+        x_sum(f, 2, part).wait_recv()
+        rows = rest[part]
+        return out[f, sy, rows].astype(F32) + rxd[f, rows].astype(F32) + rxc[f, rows].astype(F32)
+
+    @pl.loop(0, NF + Z_RELAY)
     def _(i):
-        @pl.when(i < NF)
-        def _():
-            forward(i)
-            x_sum(i, 0).start()
-            x_sum(i, 1).start()
-
-        @pl.when((i >= 1) & (i < NF + 1))
-        def _():
-            f = i - 1
-            x_sum(f, 0).wait_recv()
-            there = add(sy, way(f), G)
-            out[f, there] = (out[f, there].astype(F32) + rxf[f].astype(F32)).astype(BF)
-            x_sum(f, 2).start()
-
-        @pl.when((i >= 2) & (i < NF + 2))
-        def _():
-            f = i - 2
-            x_sum(f, 1).wait_recv()
-            x_sum(f, 2).wait_recv()
-            sx_buf[f] = (out[f, sy].astype(F32) + rxd[f].astype(F32) + rxc[f].astype(F32)).astype(BF)
+        def stage(first):
+            return pl.when((i >= first) & (i < first + NF))
+
+        @stage(0)
+        def _():
+            first = lax.rem(i, 2)
+            z_in(i, first).wait_recv()
+            z_relay(i).start()
+            for side in range(2):
+                x_own(i, row_of(first), side).start()
+            z_in(i, 1 - first).wait_recv()
+            for side in range(2):
+                x_own(i, row_of(1 - first), side).start()
+
+        @stage(FAR)
+        def _():
+            f = i - FAR
+            pass_on(f, sx)
+            z_far(f).wait_recv()
+            for side in range(2):
+                x_own(f, add(sx, 2, G), side).start()
+
+        @stage(PASS)
+        def _():
+            f = i - PASS
+            first = lax.rem(f, 2)
+            pass_on(f, row_of(first))
+            pass_on(f, row_of(1 - first))
+
+        @stage(PASS_FAR)
+        def _():
+            pass_on(i - PASS_FAR, add(sx, 2, G))
+
+        @stage(0)
+        def _():
+            for c in range(2):
+                at[i, c] = a[i, c].T
+
+        @stage(ADJOINT)
+        def _():
+            f = i - ADJOINT
+            for row in range(G):
+                x_in(f, row, 1 - lax.rem(f, 2)).wait_recv()
+                x_far(f, row).wait_recv()
+            adjoint(f)
+
+        @stage(SWEEP1)
+        def _():
+            sweep(0, i - SWEEP1, b0, p1)
+
+        @stage(SWEEP2)
+        def _():
+            sweep(1, i - SWEEP2, p1, p2)
+
+        @stage(FORWARD)
+        def _():
+            f = i - FORWARD
+            forward(f)
+            x_sum(f, 0, 0).start()
+            x_sum(f, 1, 0).start()
+
+        @stage(X_RELAY)
+        def _():
+            x_relay_sum(i - X_RELAY, 0)
+
+        @pl.when(i == OWN_ROW)
+        def _():
+            @pl.loop(0, NF)
+            def _(f):
+                x_sum(f, 0, 1).start()
+                x_sum(f, 1, 1).start()
+
+        @stage(X_TOTAL)
+        def _():
+            f = i - X_TOTAL
+            sx_buf[f, rest[0]] = x_total(f, 0).astype(BF)
             z_sum(f, 0).start()
             z_sum(f, 1).start()
 
-        @pl.when((i >= 3) & (i < NF + 3))
-        def _():
-            f = i - 3
+        @pl.when(i == OWN_RELAY)
+        def _():
+            @pl.loop(0, NF)
+            def _(f):
+                x_relay_sum(f, 1)
+
+        @stage(Z_RELAY)
+        def _():
+            f = i - Z_RELAY
             z_sum(f, 0).wait_recv()
-            there = add(sx, way(f), G)
-            sx_buf[f, there] = (sx_buf[f, there].astype(F32) + rzf[f].astype(F32)).astype(BF)
+            sx_buf[f, way(f)] = (sx_buf[f, way(f)].astype(F32) + rzf[f].astype(F32)).astype(BF)
             z_sum(f, 2).start()
 
-        @pl.when(i >= 4)
-        def _():
-            f = i - 4
-            z_sum(f, 1).wait_recv()
-            z_sum(f, 2).wait_recv()
-            fin[f] = sx_buf[f, sx].astype(F32) + rzd[f].astype(F32) + rzc[f].astype(F32)
+    @pl.loop(0, NF)
+    def _(f):
+        own = x_total(f, 1)[0]
+        z_sum(f, 1).wait_recv()
+        z_sum(f, 2).wait_recv()
+        fin[f] = own + rzd[f].astype(F32) + rzc[f].astype(F32)
 
     for kb, chunk in enumerate(swapped([fin[i // 2, i % 2] for i in range(16)], 1)):
         r2s[kb] = chunk.astype(BF)
@@ -366,6 +432,8 @@
     r2r[fq] = r2s[fq]
     for d in range(1, 16):
         a_arrival(d, r2r, bs_sem, br_sem).wait_recv()
+    for load in loads[4:]:
+        load.wait()
     halves = []
     for half in range(2):
         part = swapped([r2r[8 * half + i].astype(F32) for i in range(8)], 16)
@@ -375,22 +443,26 @@
     )
 
     for k in range(8):
-        product = dir_ref[k] + noise_ref[...] * returned[32 * k : 32 * k + 32]
-        new = res_ref[k] - step_ref[k] * product
-        new_res_ref[k] = new
+        less = step_ref[k] * (dir_ref[k] + noise_ref[...] * returned[32 * k : 32 * k + 32])
+        delta[k] = less
+        new = res_ref[k] - less
         total = jnp.sum(jnp.sum(new * new, axis=1, keepdims=True), axis=0, keepdims=True)
         ns[k : k + 1, :] = jnp.broadcast_to(total, (1, 128))
+    leave = pltpu.make_async_copy(delta, delta_hbm, out_sem)
 
     def n_copy(d):
         return remote(ns, nr.at[d], ns_sem.at[d], nr_sem.at[d], in_tiles(d))
 
     for d in range(1, 16):
         n_copy(d).start()
+    leave.start()
     norm = ns[...]
     for d in range(1, 16):
         n_copy(d).wait_recv()
         norm += nr[d]
-    norm_ref[...] = norm
+    for k in range(8):
+        norm_ref[k] = norm[k, 0]
+    leave.wait()
 
     for d in range(1, 16):
         a_exchange(d, a2s, a2r, as_sem, ar_sem).wait_send()
@@ -401,12 +473,15 @@
     def _(f):
         for side in range(2):
             z_own(f, side).wait_send()
-            x_own(f, side).wait_send()
+            for row in range(G):
+                x_own(f, row, side).wait_send()
         z_relay(f).wait_send()
-        x_relay(f).wait_send()
+        for row in range(G):
+            x_relay(f, row).wait_send()
         for kind in range(3):
-            x_sum(f, kind).wait_send()
             z_sum(f, kind).wait_send()
+            for part in range(2):
+                x_sum(f, kind, part).wait_send()
         for j in range(3):
             for side in range(4):
                 @pl.when(sides[side][0])
@@ -418,22 +493,25 @@
     spectra, noise_weight, class_map, class_kappa, solution, residual, direction, step_length, old_norm
 ):
     forward_table, back_table = tables(128, 256, NF)
-    vmem = pl.BlockSpec(memory_space=pltpu.VMEM)
     smem = pl.BlockSpec(memory_space=pltpu.SMEM)
     dma = pltpu.SemaphoreType.DMA
     field = pltpu.VMEM((NF, 2, 34 * PITCH, 128), F32)
     chunks = pltpu.VMEM((16, 32, 128), BF)
     x_part = pltpu.VMEM((NF, G, 2, 32, 128), BF)
     z_part = pltpu.VMEM((NF, 2, 32, 128), BF)
-    new_residual, norm = pl.pallas_call(
+    hbm = pl.BlockSpec(memory_space=pl.ANY)
+    delta, new_norm = pl.pallas_call(
         kernel,
         out_shape=(
             jax.ShapeDtypeStruct(residual.shape, F32),
-            jax.ShapeDtypeStruct((8, 128), F32),
+            jax.ShapeDtypeStruct((8,), F32),
         ),
-        in_specs=[vmem] * 4 + [smem] * 2 + [vmem] * 2 + [pl.BlockSpec(memory_space=pl.ANY)],
-        out_specs=(vmem, vmem),
+        in_specs=[hbm] * 6 + [smem] * 2 + [hbm],
+        out_specs=(hbm, smem),
         scratch_shapes=[
+            pltpu.VMEM(direction.shape, F32), pltpu.VMEM((32, 256), F32), pltpu.VMEM((256, 256), F32),
+            pltpu.VMEM((16, 32), jnp.int32), pltpu.VMEM((256, 256), F32), pltpu.VMEM(direction.shape, F32),
+            pltpu.VMEM(direction.shape, F32), dma((6,)), dma,
             pltpu.VMEM((NF, 2, 512, 512), BF),
             pltpu.VMEM((NF, 2, 512, 512), BF),
             pltpu.VMEM((NF, G, G, 2, 32, 128), BF),
@@ -450,19 +528,19 @@
             pltpu.VMEM((2, 512, 128), BF),
             dma((NF,)),
             dma((16,)), dma((16,)), dma((16,)), dma((16,)), dma((16,)), dma((16,)),
-            dma((NF, 3)), dma((NF, 3)), dma((NF, 3)), dma((NF, 3)),
+            dma((NF, 3)), dma((NF, 3)), dma((NF, 3, G)), dma((NF, 3, G)),
             dma((3, NF, 4)), dma((3, NF, 4)),
-            dma((NF, 3)), dma((NF, 3)), dma((NF, 3)), dma((NF, 3)),
+            dma((NF, 3, 2)), dma((NF, 3, 2)), dma((NF, 3)), dma((NF, 3)),
         ],
         compiler_params=pltpu.CompilerParams(
             collective_id=0, has_side_effects=True, vmem_limit_bytes=62 * 1024 * 1024
         ),
         name="hessian_step",
     )(
-        direction, residual, noise_weight, class_map, class_kappa, step_length,
-        jnp.asarray(forward_table), jnp.asarray(back_table), spectra.reshape(NF, 2, 512, 512),
+        direction, noise_weight, jnp.asarray(forward_table), class_map.T, jnp.asarray(back_table), residual,
+        class_kappa, step_length, spectra.reshape(NF, 2, 512, 512),
     )
-    new_norm = norm[:, 0]
+    new_residual = residual - delta
     new_solution = solution + step_length[:, None, None] * direction
     new_direction = new_residual + (new_norm / old_norm)[:, None, None] * direction
     return (new_solution, new_residual, new_direction, new_norm)

time: 122 us -> 96.9 us (0.79)
  Pallas kernels: 115 us -> 92.3 us
  local copies, waits for them, and re-layouts: 3.92 us -> 1.17 us
    pallas_call x1, Pallas kernels: 115 us -> 92.3 us  [on_device(): pl.pallas_call(kernel, out_shape=(jax.ShapeDtypeStruct(residual.shape, F3...]
    unnamed x12 -> x11, local copies, waits for them, and re-layouts: 3.13 us -> 1.17 us
where the time goes in v2:
time: 96.9 us; the launch traced here: 96.7 us
  Pallas kernels  92.3 us (95%)
  other arithmetic  2.5 us (3%)
  local copies, waits for them, and re-layouts  1.17 us (1%)
    pallas_call x1, Pallas kernels, on_device(): pl.pallas_call(kernel, out_shape=(jax.ShapeDtypeStruct(residual.shape, F3...  92.3 us

profile of v2, /device:TPU:1, one launch (start us, length us, event | category | flops | bytes accessed | tf_op | source)
XLA Modules:
  0.0 96.7 jit_solution(10102253295244525564)
XLA Ops:
  0.6 0.0 copy-start.3
  0.6 0.0 copy-start
  0.7 0.0 copy-start.1
  0.7 0.0 copy-start.4
  0.7 0.0 copy-start.2
  0.7 92.3 %hessian_step.1 = (f32[8,32,256]{2,1,0:T(8,128)}, f32[8]{0:T(128)}) custom-call(f32[8,32,256]{2,1,0:T(8,128)} %dir_hbm.1, f32[32,256]{1,0:T(8,128)} %noise_hbm.1, f32[256,256]{1,0:T(8,128)} %constant.4.clone.fwd_hbm, s32[16,32]{1,0:T(8,128)} %bitcast.3, f32[256,256]{1,0:T(8,128)} %constant.5.clone.back_hbm, f32[8,32,256]{2,1,0:T(8,128)} %res_hbm.1, ...), custom_call_target="tpu_custom_call" | custom-call | tf_op jit(solution)/shard_map/hessian_step/pallas_call | solution.py:503
  93.0 0.0 copy-done.4
  93.0 0.6 div.3
  93.7 0.0 copy-done.3
  93.7 0.0 copy-done
  93.7 0.0 copy-done.1
  93.7 0.0 copy-done.2
  93.7 1.9 %multiply_add_fusion = (f32[8,32,256]{2,1,0:T(8,128)}, f32[8,32,256]{2,1,0:T(8,128)}, f32[8,32,256]{2,1,0:T(8,128)}) fusion(f32[8,32,256]{2,1,0:T(8,128)S(1)} %copy-done, f32[8]{0:T(128)S(1)} %div.3, f32[8,32,256]{2,1,0:T(8,128)S(1)} %copy-done.1, f32[8,32,256]{2,1,0:T(8,128)} %get-tuple-element.6, f32[8,32,256]{2,1,0:T(8,128)S(1)} %copy-done.2, f32[8]{0:T(128)S(1)} %copy-done.3), kind=kLoop, calls=%fused_computation | loop fusion | flops 327680 | bytes 1835072 | tf_op jit(solution)/shard_map/add | solution.py:545
  95.5 1.1 %copy.16 = f32[8]{0:T(128)} copy(f32[8]{0:T(128)} %get-tuple-element.18) | data formatting | bytes 64
Async XLA Ops:
  0.6 93.0 %copy-start.3 = (f32[8]{0:T(128)S(1)}, f32[8]{0:T(128)}, u32[]{:S(2)}) copy-start(f32[8]{0:T(128)} %step_ref.1) | copy-start | bytes 100
  0.6 93.0 %copy-start = (f32[8,32,256]{2,1,0:T(8,128)S(1)}, f32[8,32,256]{2,1,0:T(8,128)}, u32[]{:S(2)}) copy-start(f32[8,32,256]{2,1,0:T(8,128)} %dir_hbm.1) | copy-start | bytes 786436
  0.7 93.0 %copy-start.1 = (f32[8,32,256]{2,1,0:T(8,128)S(1)}, f32[8,32,256]{2,1,0:T(8,128)}, u32[]{:S(2)}) copy-start(f32[8,32,256]{2,1,0:T(8,128)} %res_hbm.1) | copy-start | bytes 786436
  0.7 92.3 %copy-start.4 = (f32[8]{0:T(128)S(1)}, f32[8]{0:T(128)}, u32[]{:S(2)}) copy-start(f32[8]{0:T(128)} %param.19) | copy-start | bytes 100
  0.7 93.0 %copy-start.2 = (f32[8,32,256]{2,1,0:T(8,128)S(1)}, f32[8,32,256]{2,1,0:T(8,128)}, u32[]{:S(2)}) copy-start(f32[8,32,256]{2,1,0:T(8,128)} %param.15) | copy-start | bytes 786436

commit v3 on v2

v3 whole, which is shorter than its diff:
```python
import functools
import math

import jax
import jax.numpy as jnp
import numpy as np
from jax import lax
from jax.experimental import pallas as pl
from jax.experimental.pallas import tpu as pltpu
from jax.sharding import PartitionSpec as P

MESH = pl.DeviceIdType.MESH
HIGHEST = lax.Precision.HIGHEST
BF, F32 = jnp.bfloat16, jnp.float32
PITCH = 24
NF = 8
G = 4
GATHER_TURNED, SUM_TURNED = (3,), (1, 4)
FAR, PASS, PASS_FAR, ADJOINT, FORWARD, X_RELAY, X_TOTAL = 1, 2, 4, 6, 9, 12, 15
OWN_ROW, OWN_RELAY = NF + X_RELAY - 1, NF + X_TOTAL - 1
DEEP = 3
ROWS = PITCH * (32 + 2 * DEEP + 2)


def tables(freq_count, time_steps, per_block):
    freq = np.arange(freq_count)
    phase = (freq[:, None] * np.arange(time_steps)[None, :] % time_steps) * (2.0 * math.pi / time_steps)
    factor = 1.0 / math.sqrt(time_steps)
    both = np.stack([np.cos(phase), -np.sin(phase)], axis=1) * factor
    doubled = both * np.where(freq == 0, 1.0, 2.0)[:, None, None]
    forward = both.reshape(2 * freq_count, time_steps).T
    back = doubled.reshape(2 * freq_count, time_steps)
    return forward.astype(np.float32), back.astype(np.float32)


def swapped(arrays, unit):
    arrays = list(arrays)
    lane = lax.broadcasted_iota(jnp.int32, arrays[0].shape, 1)
    bit = 1
    while bit < len(arrays):
        here = ((lane // unit) & bit) != 0
        for i in range(len(arrays)):
            if i & bit == 0:
                a, c = arrays[i], arrays[i | bit]
                arrays[i] = jnp.where(here, pltpu.roll(c, bit * unit, 1), a)
                arrays[i | bit] = jnp.where(here, c, pltpu.roll(a, 128 - bit * unit, 1))
        bit *= 2
    return arrays


def row_at(x, y):
    return PITCH * (x + DEEP + 1) + y


def remote(src, dst, send, recv, device):
    return pltpu.make_async_remote_copy(
        src_ref=src, dst_ref=dst, send_sem=send, recv_sem=recv, device_id=device, device_id_type=MESH
    )


def kernel(
    dir_hbm, noise_hbm, fwd_hbm, map_hbm, back_hbm, res_hbm, kap_ref, step_ref, old_ref, spectra_ref,
    delta_hbm, norm_ref, ratio_ref,
    dir_ref, noise_ref, fwd_ref, map_ref, back_ref, res_ref, delta, in_sem, out_sem,
    a, at, q, b0, p1, p2, kd, inv, out, sx_buf, fin, a2s, a2r, r2s, r2r,
    hxs, hxr, hys, hyr, hcs, hcr, mine, near, rxf, rxd, rxc, rz, ns, nr, fh,
    a_sem, as_sem, ar_sem, bs_sem, br_sem, ns_sem, nr_sem,
    zs, zr, xs, xr, hs, hr, ms, mr, rxs, rxr, rzs, rzr,
):
    sx, sy, fq = lax.axis_index("sx"), lax.axis_index("sy"), lax.axis_index("fq")
    tile = sx * G + sy

    def add(i, d, n):
        return lax.rem(i + d + n, n)

    def on_z(d):
        return (add(sx, d, G), sy, fq)

    def on_x(d):
        return (sx, add(sy, d, G), fq)

    def in_fq(d):
        return (sx, sy, add(fq, d, 16))

    def in_tiles(d):
        other = add(tile, d, 16)
        return (other // G, lax.rem(other, G), fq)

    barrier = pltpu.get_barrier_semaphore()
    for d in range(1, 16):
        pl.semaphore_signal(barrier, inc=1, device_id=in_fq(d), device_id_type=MESH)
        pl.semaphore_signal(barrier, inc=1, device_id=in_tiles(d), device_id_type=MESH)

    loads = [
        pltpu.make_async_copy(src, dst, in_sem.at[i])
        for i, (src, dst) in enumerate((
            (dir_hbm, dir_ref), (noise_hbm, noise_ref), (fwd_hbm, fwd_ref),
            (map_hbm, map_ref), (back_hbm, back_ref), (res_hbm, res_ref),
        ))
    ]
    for load in loads:
        load.start()

    def a_copy(f):
        return pltpu.make_async_copy(spectra_ref.at[f], a.at[f], a_sem.at[f])

    for load in loads[:3]:
        load.wait()
    for f in range(NF):
        a_copy(f).start()

    weighted = (dir_ref[...] * noise_ref[...][None]).reshape(256, 256)
    spec = jnp.dot(weighted, fwd_ref[...], preferred_element_type=F32, precision=HIGHEST)
    for half in range(2):
        part = [spec[32 * k : 32 * k + 32, 128 * half : 128 * half + 128] for k in range(8)]
        for i, chunk in enumerate(swapped(part, 16)):
            a2s[8 * half + i] = chunk.astype(BF)
    pl.semaphore_wait(barrier, 30)

    def a_exchange(d, src, dst, ss, rs):
        peer = in_fq(d)
        return remote(src.at[peer[2]], dst.at[fq], ss.at[d], rs.at[d], peer)

    def a_arrival(d, dst, ss, rs):
        peer = in_fq(-d)
        return remote(dst.at[peer[2]], dst.at[peer[2]], ss.at[d], rs.at[d], peer)

    for d in range(1, 16):
        a_exchange(d, a2s, a2r, as_sem, ar_sem).start()
    a2r[fq] = a2s[fq]

    loads[3].wait()
    classes = map_ref[...]
    kappa = jnp.zeros(classes.shape, F32)
    for c in range(8):
        kappa = jnp.where(classes == c, kap_ref[c], kappa)
    scale = 1.0 / (1.0 + 4.0 * kappa)
    ratio = scale * kappa
    mine[...] = jnp.concatenate([ratio, jnp.zeros((16, 96), F32)], axis=1)
    for x in range(32):
        inv[x] = jnp.broadcast_to(scale[:, x : x + 1], (16, 128))

    around = ((-1, 0), (1, 0), (0, -1), (0, 1), (-1, -1), (1, 1), (-1, 1), (1, -1))

    def there_is(i):
        dz, dx = around[i]
        return (sx + dz >= 0) & (sx + dz < G) & (sy + dx >= 0) & (sy + dx < G)

    def tile_at(i):
        dz, dx = around[i]
        return (add(sx, dz, G), add(sy, dx, G), fq)

    def m_copy(i):
        return remote(mine, near.at[i ^ 1], ms.at[i], mr.at[i ^ 1], tile_at(i))

    def m_in(i):
        return remote(near.at[i], near.at[i], ms.at[i], mr.at[i], tile_at(i))

    for i in range(8):
        @pl.when(there_is(i))
        def _():
            m_copy(i).start()

        @pl.when(jnp.logical_not(there_is(i)))
        def _():
            near[i] = jnp.zeros((16, 128), F32)

    @pl.loop(0, NF)
    def _(f):
        b0[f] = jnp.zeros((2, ROWS, 128), F32)

    for f in range(NF):
        a_copy(f).wait()
    for d in range(1, 16):
        a_arrival(d, a2r, as_sem, ar_sem).wait_recv()
    for i, block in enumerate(swapped([a2r[kb].astype(F32) for kb in range(16)], 1)):
        q[i // 2, sx, sy, i % 2] = block.astype(BF)

    def order_of(freqs):
        def pick(f, straight, other):
            turned = sum(((f == t).astype(jnp.int32) for t in freqs), jnp.int32(0))
            return straight + turned * (other - straight)

        def along(f, d, second):
            on_sx = pick(f, 0, d) if second else pick(f, d, 0)
            return (add(sx, on_sx, G), add(sy, d - on_sx, G), fq)

        def ones(f, d):
            return add(pick(f, sx, sy), d, G)

        def twos(f, d):
            return add(pick(f, sy, sx), d, G)

        return pick, along, ones, twos

    pick, along, ones, twos = order_of(GATHER_TURNED)
    s_pick, s_along, s_ones, s_twos = order_of(SUM_TURNED)

    def block_at(f, one, two):
        return q.at[f, pick(f, one, two), pick(f, two, one)]

    def g_copy(f, block, send, recv, d, second):
        return remote(block, block, send, recv, along(f, d, second))

    def z_own(f, side):
        return g_copy(f, q.at[f, sx, sy], zs.at[f, side], zr.at[f, side], 1 + 2 * side, False)

    def z_in(f, side):
        block = block_at(f, ones(f, 3 + 2 * side), twos(f, 0))
        return g_copy(f, block, zs.at[f, side], zr.at[f, side], 1, False)

    def z_across(f):
        return g_copy(f, q.at[f, sx, sy], zs.at[f, 2], zr.at[f, 2], 2, False)

    def z_far(f):
        block = block_at(f, ones(f, 2), twos(f, 0))
        return g_copy(f, block, zs.at[f, 2], zr.at[f, 2], 2, False)

    def x_own(f, row, side):
        block = block_at(f, row, twos(f, 0))
        return g_copy(f, block, xs.at[f, side, row], xr.at[f, side, row], 1 + 2 * side, True)

    def x_relay(f, row):
        side = lax.rem(f, 2)
        block = block_at(f, row, twos(f, 3 + 2 * side))
        return g_copy(f, block, xs.at[f, 2, row], xr.at[f, 2, row], 1 + 2 * side, True)

    def x_in(f, row, side):
        block = block_at(f, row, twos(f, 3 + 2 * side))
        return g_copy(f, block, xs.at[f, side, row], xr.at[f, side, row], 1, True)

    def x_far(f, row):
        block = block_at(f, row, twos(f, 2))
        return g_copy(f, block, xs.at[f, 2, row], xr.at[f, 2, row], 1, True)

    def h_bufs(i):
        return (hxs, hxr, i) if i < 2 else (hys, hyr, i - 2) if i < 4 else (hcs, hcr, i - 4)

    def h_out(f, i):
        s, r, k = h_bufs(i)
        return remote(s.at[f, k], r.at[f, k ^ 1], hs.at[f, i], hr.at[f, i ^ 1], tile_at(i))

    def h_in(f, i):
        _, r, k = h_bufs(i)
        return remote(r.at[f, k], r.at[f, k], hs.at[f, i], hr.at[f, i], tile_at(i))

    def corner(i, inside):
        dz, dx = around[i]
        x0 = (0 if dz < 0 else 30) if inside else (-2 if dz < 0 else 32)
        y0 = (0 if dx < 0 else 14) if inside else (-2 if dx < 0 else 16)
        return [(4 * c + 2 * m + n, c, row_at(x0 + m, y0 + n)) for c in range(2) for m in range(2) for n in range(2)]

    def send_edges(f):
        for c in range(2):
            for m in range(DEEP):
                hxs[f, 0, c, m] = b0[f, c, pl.ds(row_at(m, 0), 16), :].astype(BF)
                hxs[f, 1, c, m] = b0[f, c, pl.ds(row_at(32 - DEEP + m, 0), 16), :].astype(BF)
                hys[f, 0, c, m] = b0[f, c, pl.ds(row_at(0, m), 32, stride=PITCH), :].astype(BF)
                hys[f, 1, c, m] = b0[f, c, pl.ds(row_at(0, 16 - DEEP + m), 32, stride=PITCH), :].astype(BF)
        for i in range(4, 8):
            for to, c, at_row in corner(i, True):
                hcs[f, i - 4, to : to + 1, :] = b0[f, c, at_row : at_row + 1, :]
        for i in range(8):
            @pl.when(there_is(i))
            def _():
                h_out(f, i).start()

    def take_halos(f):
        for i in range(8):
            @pl.when(there_is(i))
            def _():
                h_in(f, i).wait_recv()
                for c in range(2):
                    for m in range(DEEP):
                        if i < 2:
                            x = m + (-DEEP, 32)[i]
                            b0[f, c, pl.ds(row_at(x, 0), 16), :] = hxr[f, i, c, m].astype(F32)
                        elif i < 4:
                            y = m + (-DEEP, 16)[i - 2]
                            b0[f, c, pl.ds(row_at(0, y), 32, stride=PITCH), :] = hyr[f, i - 2, c, m].astype(F32)
                if i >= 4:
                    for at, c, at_row in corner(i, False):
                        b0[f, c, at_row : at_row + 1, :] = hcr[f, i - 4, at : at + 1, :]

    def adjoint(f):
        real = q[f, :, :, 0].reshape(512, 128)
        imag = q[f, :, :, 1].reshape(512, 128)
        acc = jnp.dot(a[f, 0], jnp.concatenate([real, imag], axis=1), preferred_element_type=F32)
        acc += jnp.dot(a[f, 1], jnp.concatenate([imag, -real], axis=1), preferred_element_type=F32)
        for x in range(32):
            for c in range(2):
                b0[f, c, pl.ds(row_at(x, 0), 16), :] = (
                    acc[16 * x : 16 * x + 16, 128 * c : 128 * c + 128] * inv[x]
                )
        send_edges(f)

    @pl.loop(0, NF)
    def _(f):
        for side in range(2):
            z_own(f, side).start()
        z_across(f).start()
        for side in range(2):
            x_own(f, ones(f, 0), side).start()

    for i in range(8):
        @pl.when(there_is(i))
        def _():
            m_in(i).wait_recv()
    maps = {d: near[i] for i, d in enumerate(around)}
    maps[0, 0] = mine[...]
    line = lax.broadcasted_iota(jnp.int32, (8, 128), 0)

    def cells(x, dx, rows):
        dz = -1 if x < 0 else 1 if x > 31 else 0
        x -= 32 * dz
        return jnp.broadcast_to(maps[dz, dx][rows, x : x + 1], (rows.stop - rows.start, 128))

    for x in range(-DEEP, 32 + DEEP):
        kd[pl.ds(row_at(x, 0), 16), :] = cells(x, 0, slice(0, 16))
        rim = jnp.where(line < DEEP, cells(x, 1, slice(0, 8)), 0.0)
        if x < 31 + DEEP:
            rim = jnp.where(line >= 8 - DEEP, cells(x + 1, -1, slice(8, 16)), rim)
        kd[pl.ds(row_at(x, 16), 8), :] = rim
    for start in (0, ROWS - PITCH):
        kd[pl.ds(start, PITCH), :] = jnp.zeros((PITCH, 128), F32)
    kd[pl.ds(16, 8), :] = jnp.where(line >= 8 - DEEP, cells(-DEEP, -1, slice(8, 16)), 0.0)

    def pass_on(f, row):
        x_in(f, row, lax.rem(f, 2)).wait_recv()
        x_relay(f, row).start()

    def row_of(f, side):
        return ones(f, 3 + 2 * side)

    def swept(f, c, start, size, p):
        beside = (
            p[c, pl.ds(start - PITCH, size), :] + p[c, pl.ds(start + PITCH, size), :]
            + p[c, pl.ds(start - 1, size), :] + p[c, pl.ds(start + 1, size), :]
        )
        return b0[f, c, pl.ds(start, size), :] + kd[pl.ds(start, size), :] * beside

    def sweep(f, before, after, layers):
        low = row_at(-layers, -layers) // 8 * 8
        high = -(-row_at(31 + layers, 16 + layers) // 8) * 8
        for start in range(low, high, 16):
            size = min(16, high - start)
            for c in range(2):
                after[c, pl.ds(start, size), :] = swept(f, c, start, size, before)

    def forward(f):
        take_halos(f)
        sweep(f, b0.at[f], p1, 2)
        sweep(f, p1, p2, 1)
        for x in range(32):
            for c in range(2):
                fh[c, pl.ds(16 * x, 16), :] = swept(f, c, row_at(x, 0), 16, p2).astype(BF)
        real, imag = fh[0], fh[1]
        acc = jnp.dot(at[f, 0], jnp.concatenate([real, imag], axis=1), preferred_element_type=F32)
        acc += jnp.dot(at[f, 1], jnp.concatenate([-imag, real], axis=1), preferred_element_type=F32)
        for t in range(16):
            for c in range(2):
                there = s_pick(f, t % G, t // G)
                row = lax.rem(s_pick(f, t // G, t % G) + G - s_ones(f, 0), G)
                out[f, there, row, c] = acc[32 * t : 32 * t + 32, 128 * c : 128 * c + 128].astype(BF)

    def way(f):
        return 1 + 2 * lax.rem(f, 2)

    def back(f):
        return 3 - 2 * lax.rem(f, 2)

    rest = (pl.ds(1, G - 1), pl.ds(0, 1))

    def x_sum(f, kind, part):
        d, to, land = ((2, way(f), rxf), (back(f), back(f), rxd), (way(f), way(f), rxc))[kind]
        return remote(
            out.at[f, s_twos(f, d), rest[part]], land.at[f, rest[part]],
            rxs.at[f, kind, part], rxr.at[f, kind, part], s_along(f, to, True),
        )

    def z_sum(f, d):
        return remote(sx_buf.at[f, d], rz.at[f, d], rzs.at[f, d], rzr.at[f, d], s_along(f, d, False))

    def x_relay_sum(f, part):
        x_sum(f, 0, part).wait_recv()
        there, rows = s_twos(f, way(f)), rest[part]
        out[f, there, rows] = (out[f, there, rows].astype(F32) + rxf[f, rows].astype(F32)).astype(BF)
        x_sum(f, 2, part).start()

    def x_total(f, part):
        x_sum(f, 1, part).wait_recv()
        x_sum(f, 2, part).wait_recv()
        rows = rest[part]
        return out[f, s_twos(f, 0), rows].astype(F32) + rxd[f, rows].astype(F32) + rxc[f, rows].astype(F32)

    @pl.loop(0, NF + X_TOTAL)
    def _(i):
        def stage(first):
            return pl.when((i >= first) & (i < first + NF))

        @stage(0)
        def _():
            first = lax.rem(i, 2)
            z_in(i, first).wait_recv()
            for side in range(2):
                x_own(i, row_of(i, first), side).start()
            z_in(i, 1 - first).wait_recv()
            for side in range(2):
                x_own(i, row_of(i, 1 - first), side).start()

        @stage(FAR)
        def _():
            f = i - FAR
            pass_on(f, ones(f, 0))
            z_far(f).wait_recv()
            for side in range(2):
                x_own(f, ones(f, 2), side).start()

        @stage(PASS)
        def _():
            f = i - PASS
            first = lax.rem(f, 2)
            pass_on(f, row_of(f, first))
            pass_on(f, row_of(f, 1 - first))

        @stage(PASS_FAR)
        def _():
            f = i - PASS_FAR
            pass_on(f, ones(f, 2))

        @stage(0)
        def _():
            for c in range(2):
                at[i, c] = a[i, c].T

        @stage(ADJOINT)
        def _():
            f = i - ADJOINT
            for row in range(G):
                x_in(f, row, 1 - lax.rem(f, 2)).wait_recv()
                x_far(f, row).wait_recv()
            adjoint(f)

        @stage(FORWARD)
        def _():
            f = i - FORWARD
            forward(f)
            x_sum(f, 0, 0).start()
            x_sum(f, 1, 0).start()

        @stage(X_RELAY)
        def _():
            x_relay_sum(i - X_RELAY, 0)

        @pl.when(i == OWN_ROW)
        def _():
            @pl.loop(0, NF)
            def _(f):
                x_sum(f, 0, 1).start()
                x_sum(f, 1, 1).start()

        @stage(X_TOTAL)
        def _():
            f = i - X_TOTAL
            sx_buf[f, rest[0]] = x_total(f, 0).astype(BF)
            for d in range(1, G):
                z_sum(f, d).start()

        @pl.when(i == OWN_RELAY)
        def _():
            @pl.loop(0, NF)
            def _(f):
                x_relay_sum(f, 1)

    @pl.loop(0, NF)
    def _(f):
        total = x_total(f, 1)[0]
        for d in range(1, G):
            z_sum(f, d).wait_recv()
            total += rz[f, d].astype(F32)
        fin[f] = total

    for kb, chunk in enumerate(swapped([fin[i // 2, i % 2] for i in range(16)], 1)):
        r2s[kb] = chunk.astype(BF)
    for d in range(1, 16):
        a_exchange(d, r2s, r2r, bs_sem, br_sem).start()
    r2r[fq] = r2s[fq]
    for d in range(1, 16):
        a_arrival(d, r2r, bs_sem, br_sem).wait_recv()
    for load in loads[4:]:
        load.wait()
    halves = []
    for half in range(2):
        part = swapped([r2r[8 * half + i].astype(F32) for i in range(8)], 16)
        halves.append(jnp.concatenate(part, axis=0))
    returned = jnp.dot(
        jnp.concatenate(halves, axis=1), back_ref[...], preferred_element_type=F32, precision=HIGHEST
    )

    for k in range(8):
        less = step_ref[k] * (dir_ref[k] + noise_ref[...] * returned[32 * k : 32 * k + 32])
        delta[k] = less
        new = res_ref[k] - less
        total = jnp.sum(jnp.sum(new * new, axis=1, keepdims=True), axis=0, keepdims=True)
        ns[k : k + 1, :] = jnp.broadcast_to(total, (1, 128))
    leave = pltpu.make_async_copy(delta, delta_hbm, out_sem)

    def n_copy(d):
        return remote(ns, nr.at[d], ns_sem.at[d], nr_sem.at[d], in_tiles(d))

    for d in range(1, 16):
        n_copy(d).start()
    leave.start()
    norm = ns[...]
    for d in range(1, 16):
        n_copy(d).wait_recv()
        norm += nr[d]
    column = lax.broadcasted_iota(jnp.int32, (8, 128), 0)
    old = jnp.ones((8, 128), F32)
    for k in range(8):
        old = jnp.where(column == k, old_ref[k], old)
    growth = norm / old
    for k in range(8):
        norm_ref[k] = norm[k, 0]
        ratio_ref[k] = growth[k, 0]
    leave.wait()

    for d in range(1, 16):
        a_exchange(d, a2s, a2r, as_sem, ar_sem).wait_send()
        a_exchange(d, r2s, r2r, bs_sem, br_sem).wait_send()
        n_copy(d).wait_send()

    @pl.loop(0, NF)
    def _(f):
        for side in range(2):
            z_own(f, side).wait_send()
            for row in range(G):
                x_own(f, row, side).wait_send()
        z_across(f).wait_send()
        for row in range(G):
            x_relay(f, row).wait_send()
        for d in range(1, G):
            z_sum(f, d).wait_send()
        for kind in range(3):
            for part in range(2):
                x_sum(f, kind, part).wait_send()
        for i in range(8):
            @pl.when(there_is(i))
            def _():
                h_out(f, i).wait_send()

    for i in range(8):
        @pl.when(there_is(i))
        def _():
            m_copy(i).wait_send()


def on_device(
    spectra, noise_weight, class_map, class_kappa, solution, residual, direction, step_length, old_norm
):
    forward_table, back_table = tables(128, 256, NF)
    smem = pl.BlockSpec(memory_space=pltpu.SMEM)
    dma = pltpu.SemaphoreType.DMA
    field = pltpu.VMEM((2, ROWS, 128), F32)
    chunks = pltpu.VMEM((16, 32, 128), BF)
    x_part = pltpu.VMEM((NF, G, 2, 32, 128), BF)
    hbm = pl.BlockSpec(memory_space=pl.ANY)
    delta, norm, growth = pl.pallas_call(
        kernel,
        out_shape=(
            jax.ShapeDtypeStruct(residual.shape, F32),
            jax.ShapeDtypeStruct((8,), F32),
            jax.ShapeDtypeStruct((8,), F32),
        ),
        in_specs=[hbm] * 6 + [smem] * 3 + [hbm],
        out_specs=(hbm, smem, smem),
        scratch_shapes=[
            pltpu.VMEM(direction.shape, F32), pltpu.VMEM((32, 256), F32), pltpu.VMEM((256, 256), F32),
            pltpu.VMEM((16, 32), jnp.int32), pltpu.VMEM((256, 256), F32), pltpu.VMEM(direction.shape, F32),
            pltpu.VMEM(direction.shape, F32), dma((6,)), dma,
            pltpu.VMEM((NF, 2, 512, 512), BF),
            pltpu.VMEM((NF, 2, 512, 512), BF),
            pltpu.VMEM((NF, G, G, 2, 32, 128), BF),
            pltpu.VMEM((NF, 2, ROWS, 128), F32), field, field,
            pltpu.VMEM((ROWS, 128), F32), pltpu.VMEM((32, 16, 128), F32),
            pltpu.VMEM((NF, G, G, 2, 32, 128), BF),
            x_part,
            pltpu.VMEM((NF, 2, 32, 128), F32),
            chunks, chunks, chunks, chunks,
            pltpu.VMEM((NF, 2, 2, DEEP, 16, 128), BF), pltpu.VMEM((NF, 2, 2, DEEP, 16, 128), BF),
            pltpu.VMEM((NF, 2, 2, DEEP, 32, 128), BF), pltpu.VMEM((NF, 2, 2, DEEP, 32, 128), BF),
            pltpu.VMEM((NF, 4, 8, 128), F32), pltpu.VMEM((NF, 4, 8, 128), F32),
            pltpu.VMEM((16, 128), F32), pltpu.VMEM((8, 16, 128), F32),
            x_part, x_part, x_part, x_part,
            pltpu.VMEM((8, 128), F32), pltpu.VMEM((16, 8, 128), F32),
            pltpu.VMEM((2, 512, 128), BF),
            dma((NF,)),
            dma((16,)), dma((16,)), dma((16,)), dma((16,)), dma((16,)), dma((16,)),
            dma((NF, 3)), dma((NF, 3)), dma((NF, 3, G)), dma((NF, 3, G)),
            dma((NF, 8)), dma((NF, 8)), dma((8,)), dma((8,)),
            dma((NF, 3, 2)), dma((NF, 3, 2)), dma((NF, G)), dma((NF, G)),
        ],
        compiler_params=pltpu.CompilerParams(
            collective_id=0, has_side_effects=True, vmem_limit_bytes=62 * 1024 * 1024
        ),
        name="hessian_step",
    )(
        direction, noise_weight, jnp.asarray(forward_table), class_map.T, jnp.asarray(back_table), residual,
        class_kappa, step_length, old_norm, spectra.reshape(NF, 2, 512, 512),
    )
    new_residual = residual - delta
    new_norm = jnp.maximum(norm, 0.0)
    new_solution = solution + step_length[:, None, None] * direction
    new_direction = new_residual + growth[:, None, None] * direction
    return (new_solution, new_residual, new_direction, new_norm)


def solution(mesh):
    columns = P("fq", ("sx", "sy"), None)
    return jax.shard_map(
        on_device,
        mesh=mesh,
        in_specs=(
            P("fq", None, "sx", "sy", None), P(("sx", "sy"), None), P("sx", "sy"), P(),
            columns, columns, columns, P("fq"), P("fq"),
        ),
        out_specs=(columns, columns, columns, P("fq")),
        check_vma=False,
    )
```

time: 96.9 us -> 90.3 us (0.932)
  Pallas kernels: 92.3 us -> 86.5 us
  local copies, waits for them, and re-layouts: 1.17 us -> 0.02 us
    pallas_call x1, Pallas kernels: 92.3 us -> 86.5 us  [on_device(): pl.pallas_call(kernel, out_shape=(jax.ShapeDtypeStruct(residual.shape, F3...]
    unnamed x11 -> x8, local copies, waits for them, and re-layouts: 1.17 us -> 0.02 us
    max x0 -> x1, other arithmetic: none -> 1.12 us  [on_device(): new_norm = jnp.maximum(norm, 0.0)]
where the time goes in v3:
time: 90.3 us; the launch traced here: 90.2 us
  Pallas kernels  86.5 us (96%)
  other arithmetic  2.98 us (3%)
    pallas_call x1, Pallas kernels, on_device(): pl.pallas_call(kernel, out_shape=(jax.ShapeDtypeStruct(residual.shape, F3...  86.5 us
    add x1, other arithmetic, on_device(): new_direction = new_residual + growth[:, None, None] * direction  1.86 us

profile of v3, /device:TPU:1, one launch (start us, length us, event | category | flops | bytes accessed | tf_op | source)
XLA Modules:
  0.0 90.2 jit_solution(9644997505893599989)
XLA Ops:
  0.6 0.0 copy-start.3
  0.6 0.0 copy-start
  0.7 0.0 copy-start.1
  0.7 0.0 copy-start.2
  0.7 86.5 %hessian_step.1 = (f32[8,32,256]{2,1,0:T(8,128)}, f32[8]{0:T(128)}, f32[8]{0:T(128)}) custom-call(f32[8,32,256]{2,1,0:T(8,128)} %dir_hbm.1, f32[32,256]{1,0:T(8,128)} %noise_hbm.1, f32[256,256]{1,0:T(8,128)} %constant.6.clone.fwd_hbm, s32[16,32]{1,0:T(8,128)} %bitcast.3, f32[256,256]{1,0:T(8,128)} %constant.7.clone.back_hbm, f32[8,32,256]{2,1,0:T(8,128)} %res_hbm.1, ...), custom_call_target="tpu_custom_call" | custom-call | tf_op jit(solution)/shard_map/hessian_step/pallas_call | solution.py:568
  87.2 1.1 %broadcast_maximum_fusion = f32[8]{0:T(128)} fusion(f32[8]{0:T(128)} %get-tuple-element.9), kind=kLoop, calls=%fused_computation.2 | loop fusion | flops 8 | bytes 64 | tf_op jit(solution)/shard_map/max | solution.py:612
  88.3 0.0 copy-done.3
  88.3 0.0 copy-done
  88.3 0.0 copy-done.1
  88.3 0.0 copy-done.2
  88.3 1.9 %multiply_add_fusion = (f32[8,32,256]{2,1,0:T(8,128)}, f32[8,32,256]{2,1,0:T(8,128)}, f32[8,32,256]{2,1,0:T(8,128)}) fusion(f32[8,32,256]{2,1,0:T(8,128)S(1)} %copy-done, f32[8]{0:T(128)} %get-tuple-element.8, f32[8,32,256]{2,1,0:T(8,128)S(1)} %copy-done.1, f32[8,32,256]{2,1,0:T(8,128)} %get-tuple-element.7, f32[8,32,256]{2,1,0:T(8,128)S(1)} %copy-done.2, ...), kind=kLoop, calls=%fused_computation | loop fusion | flops 327680 | bytes 1835072 | tf_op jit(solution)/shard_map/add | solution.py:614
Async XLA Ops:
  0.6 87.6 %copy-start.3 = (f32[8]{0:T(128)S(1)}, f32[8]{0:T(128)}, u32[]{:S(2)}) copy-start(f32[8]{0:T(128)} %step_ref.1) | copy-start | bytes 100
  0.6 87.6 %copy-start = (f32[8,32,256]{2,1,0:T(8,128)S(1)}, f32[8,32,256]{2,1,0:T(8,128)}, u32[]{:S(2)}) copy-start(f32[8,32,256]{2,1,0:T(8,128)} %dir_hbm.1) | copy-start | bytes 786436
  0.7 87.6 %copy-start.1 = (f32[8,32,256]{2,1,0:T(8,128)S(1)}, f32[8,32,256]{2,1,0:T(8,128)}, u32[]{:S(2)}) copy-start(f32[8,32,256]{2,1,0:T(8,128)} %res_hbm.1) | copy-start | bytes 786436
  0.7 87.6 %copy-start.2 = (f32[8,32,256]{2,1,0:T(8,128)S(1)}, f32[8,32,256]{2,1,0:T(8,128)}, u32[]{:S(2)}) copy-start(f32[8,32,256]{2,1,0:T(8,128)} %param.15) | copy-start | bytes 786436

commit v4 on v3

--- a/solution.py
+++ b/solution.py
@@ -15,7 +15,7 @@
 PITCH = 24
 NF = 8
 G = 4
-GATHER_TURNED, SUM_TURNED = (3,), (1, 4)
+GATHER_TURNED, SUM_TURNED = (3,), (0, 3)
 FAR, PASS, PASS_FAR, ADJOINT, FORWARD, X_RELAY, X_TOTAL = 1, 2, 4, 6, 9, 12, 15
 OWN_ROW, OWN_RELAY = NF + X_RELAY - 1, NF + X_TOTAL - 1
 DEEP = 3
@@ -511,24 +511,10 @@
     for d in range(1, 16):
         n_copy(d).start()
     leave.start()
-    norm = ns[...]
-    for d in range(1, 16):
-        n_copy(d).wait_recv()
-        norm += nr[d]
-    column = lax.broadcasted_iota(jnp.int32, (8, 128), 0)
-    old = jnp.ones((8, 128), F32)
-    for k in range(8):
-        old = jnp.where(column == k, old_ref[k], old)
-    growth = norm / old
-    for k in range(8):
-        norm_ref[k] = norm[k, 0]
-        ratio_ref[k] = growth[k, 0]
-    leave.wait()
 
     for d in range(1, 16):
         a_exchange(d, a2s, a2r, as_sem, ar_sem).wait_send()
         a_exchange(d, r2s, r2r, bs_sem, br_sem).wait_send()
-        n_copy(d).wait_send()
 
     @pl.loop(0, NF)
     def _(f):
@@ -553,6 +539,22 @@
         @pl.when(there_is(i))
         def _():
             m_copy(i).wait_send()
+
+    norm = ns[...]
+    for d in range(1, 16):
+        n_copy(d).wait_recv()
+        norm += nr[d]
+    column = lax.broadcasted_iota(jnp.int32, (8, 128), 0)
+    old = jnp.ones((8, 128), F32)
+    for k in range(8):
+        old = jnp.where(column == k, old_ref[k], old)
+    growth = norm / old
+    for k in range(8):
+        norm_ref[k] = norm[k, 0]
+        ratio_ref[k] = growth[k, 0]
+    leave.wait()
+    for d in range(1, 16):
+        n_copy(d).wait_send()
 
 
 def on_device(

time: 90.3 us -> 89.8 us (level)
  no operation moved by 1% of the time
where the time goes in v4:
time: 89.8 us; the launch traced here: 89.6 us
  Pallas kernels  85.9 us (96%)
  other arithmetic  2.98 us (3%)
    pallas_call x1, Pallas kernels, on_device(): pl.pallas_call(kernel, out_shape=(jax.ShapeDtypeStruct(residual.shape, F3...  85.9 us
    add x1, other arithmetic, on_device(): new_direction = new_residual + growth[:, None, None] * direction  1.86 us

profile of v4, /device:TPU:1, one launch (start us, length us, event | category | flops | bytes accessed | tf_op | source)
XLA Modules:
  0.0 89.6 jit_solution(16808535947555718730)
XLA Ops:
  0.6 0.0 copy-start.3
  0.6 0.0 copy-start
  0.7 0.0 copy-start.1
  0.7 0.0 copy-start.2
  0.7 85.9 %hessian_step.1 = (f32[8,32,256]{2,1,0:T(8,128)}, f32[8]{0:T(128)}, f32[8]{0:T(128)}) custom-call(f32[8,32,256]{2,1,0:T(8,128)} %dir_hbm.1, f32[32,256]{1,0:T(8,128)} %noise_hbm.1, f32[256,256]{1,0:T(8,128)} %constant.6.clone.fwd_hbm, s32[16,32]{1,0:T(8,128)} %bitcast.3, f32[256,256]{1,0:T(8,128)} %constant.7.clone.back_hbm, f32[8,32,256]{2,1,0:T(8,128)} %res_hbm.1, ...), custom_call_target="tpu_custom_call" | custom-call | tf_op jit(solution)/shard_map/hessian_step/pallas_call | solution.py:570
  86.6 1.1 %broadcast_maximum_fusion = f32[8]{0:T(128)} fusion(f32[8]{0:T(128)} %get-tuple-element.9), kind=kLoop, calls=%fused_computation.2 | loop fusion | flops 8 | bytes 64 | tf_op jit(solution)/shard_map/max | solution.py:614
  87.7 0.0 copy-done.3
  87.7 0.0 copy-done
  87.7 0.0 copy-done.1
  87.8 0.0 copy-done.2
  87.8 1.9 %multiply_add_fusion = (f32[8,32,256]{2,1,0:T(8,128)}, f32[8,32,256]{2,1,0:T(8,128)}, f32[8,32,256]{2,1,0:T(8,128)}) fusion(f32[8,32,256]{2,1,0:T(8,128)S(1)} %copy-done, f32[8]{0:T(128)} %get-tuple-element.8, f32[8,32,256]{2,1,0:T(8,128)S(1)} %copy-done.1, f32[8,32,256]{2,1,0:T(8,128)} %get-tuple-element.7, f32[8,32,256]{2,1,0:T(8,128)S(1)} %copy-done.2, ...), kind=kLoop, calls=%fused_computation | loop fusion | flops 327680 | bytes 1835072 | tf_op jit(solution)/shard_map/add | solution.py:616
Async XLA Ops:
  0.6 87.1 %copy-start.3 = (f32[8]{0:T(128)S(1)}, f32[8]{0:T(128)}, u32[]{:S(2)}) copy-start(f32[8]{0:T(128)} %step_ref.1) | copy-start | bytes 100
  0.6 87.1 %copy-start = (f32[8,32,256]{2,1,0:T(8,128)S(1)}, f32[8,32,256]{2,1,0:T(8,128)}, u32[]{:S(2)}) copy-start(f32[8,32,256]{2,1,0:T(8,128)} %dir_hbm.1) | copy-start | bytes 786436
  0.7 87.1 %copy-start.1 = (f32[8,32,256]{2,1,0:T(8,128)S(1)}, f32[8,32,256]{2,1,0:T(8,128)}, u32[]{:S(2)}) copy-start(f32[8,32,256]{2,1,0:T(8,128)} %res_hbm.1) | copy-start | bytes 786436
  0.7 87.1 %copy-start.2 = (f32[8,32,256]{2,1,0:T(8,128)S(1)}, f32[8,32,256]{2,1,0:T(8,128)}, u32[]{:S(2)}) copy-start(f32[8,32,256]{2,1,0:T(8,128)} %param.15) | copy-start | bytes 786436

commit v5 on v4

--- a/solution.py
+++ b/solution.py
@@ -98,7 +98,7 @@
             (map_hbm, map_ref), (back_hbm, back_ref), (res_hbm, res_ref),
         ))
     ]
-    for load in loads:
+    for load in loads[:3]:
         load.start()
 
     def a_copy(f):
@@ -106,6 +106,8 @@
 
     for load in loads[:3]:
         load.wait()
+    for load in loads[3:]:
+        load.start()
     for f in range(NF):
         a_copy(f).start()
 

time: 89.8 us -> 89.6 us (level)
  no operation moved by 1% of the time
where the time goes in v5:
time: 89.6 us; the launch traced here: 89.5 us
  Pallas kernels  85.8 us (96%)
  other arithmetic  2.98 us (3%)
    pallas_call x1, Pallas kernels, on_device(): pl.pallas_call(kernel, out_shape=(jax.ShapeDtypeStruct(residual.shape, F3...  85.8 us
    add x1, other arithmetic, on_device(): new_direction = new_residual + growth[:, None, None] * direction  1.86 us

profile of v5, /device:TPU:1, one launch (start us, length us, event | category | flops | bytes accessed | tf_op | source)
XLA Modules:
  0.0 89.5 jit_solution(10749173892049546945)
XLA Ops:
  0.6 0.0 copy-start.3
  0.6 0.0 copy-start
  0.7 0.0 copy-start.1
  0.7 0.0 copy-start.2
  0.7 85.8 %hessian_step.1 = (f32[8,32,256]{2,1,0:T(8,128)}, f32[8]{0:T(128)}, f32[8]{0:T(128)}) custom-call(f32[8,32,256]{2,1,0:T(8,128)} %dir_hbm.1, f32[32,256]{1,0:T(8,128)} %noise_hbm.1, f32[256,256]{1,0:T(8,128)} %constant.6.clone.fwd_hbm, s32[16,32]{1,0:T(8,128)} %bitcast.3, f32[256,256]{1,0:T(8,128)} %constant.7.clone.back_hbm, f32[8,32,256]{2,1,0:T(8,128)} %res_hbm.1, ...), custom_call_target="tpu_custom_call" | custom-call | tf_op jit(solution)/shard_map/hessian_step/pallas_call | solution.py:572
  86.5 1.1 %broadcast_maximum_fusion = f32[8]{0:T(128)} fusion(f32[8]{0:T(128)} %get-tuple-element.9), kind=kLoop, calls=%fused_computation.2 | loop fusion | flops 8 | bytes 64 | tf_op jit(solution)/shard_map/max | solution.py:616
  87.6 0.0 copy-done.3
  87.6 0.0 copy-done
  87.6 0.0 copy-done.1
  87.6 0.0 copy-done.2
  87.6 1.9 %multiply_add_fusion = (f32[8,32,256]{2,1,0:T(8,128)}, f32[8,32,256]{2,1,0:T(8,128)}, f32[8,32,256]{2,1,0:T(8,128)}) fusion(f32[8,32,256]{2,1,0:T(8,128)S(1)} %copy-done, f32[8]{0:T(128)} %get-tuple-element.8, f32[8,32,256]{2,1,0:T(8,128)S(1)} %copy-done.1, f32[8,32,256]{2,1,0:T(8,128)} %get-tuple-element.7, f32[8,32,256]{2,1,0:T(8,128)S(1)} %copy-done.2, ...), kind=kLoop, calls=%fused_computation | loop fusion | flops 327680 | bytes 1835072 | tf_op jit(solution)/shard_map/add | solution.py:618
Async XLA Ops:
  0.6 87.0 %copy-start.3 = (f32[8]{0:T(128)S(1)}, f32[8]{0:T(128)}, u32[]{:S(2)}) copy-start(f32[8]{0:T(128)} %step_ref.1) | copy-start | bytes 100
  0.6 87.0 %copy-start = (f32[8,32,256]{2,1,0:T(8,128)S(1)}, f32[8,32,256]{2,1,0:T(8,128)}, u32[]{:S(2)}) copy-start(f32[8,32,256]{2,1,0:T(8,128)} %dir_hbm.1) | copy-start | bytes 786436
  0.7 87.0 %copy-start.1 = (f32[8,32,256]{2,1,0:T(8,128)S(1)}, f32[8,32,256]{2,1,0:T(8,128)}, u32[]{:S(2)}) copy-start(f32[8,32,256]{2,1,0:T(8,128)} %res_hbm.1) | copy-start | bytes 786436
  0.7 87.0 %copy-start.2 = (f32[8,32,256]{2,1,0:T(8,128)S(1)}, f32[8,32,256]{2,1,0:T(8,128)}, u32[]{:S(2)}) copy-start(f32[8,32,256]{2,1,0:T(8,128)} %param.15) | copy-start | bytes 786436
